TPU v7x, 256 devices: a whole 4x4x8 slice. The times are simulated.
256 devices in a mesh: shell: 16 (over x, z_lo, core), sky: 16 (over y, z_hi).
Axes of the slice: x: 4, y: 4, z: 8 (z_hi: 4, z_lo: 2; z = z_hi * 2 + z_lo), core: 2. Of those that a mesh axis runs over, the one named last changes fastest.
Arguments:
- coords: int32 [3, 16, 16, 512], P(None, 'shell', 'sky'), may hold values from 0 to 4095, as said below
- weights: bfloat16 [16, 16, 512], P('shell', 'sky'), may hold values from 0.5 to 2
- live: int32 [16, 16], P('shell', 'sky'), may hold values from 128 to 512, as said below
Outputs:
- jackknife: float32 [16, 128, 600], P('shell', 'sky')
Inputs may be any that keep to these rules, and one draw needn't show every extreme that they name: On device (a, b), coords[0] lies in [a * 256, (a+1) * 256), coords[1] in [b * 256, (b+1) * 256), coords[2] in [0, 1024). `live`: live slots are the first ones of a device; some device is full in every draw.
All inputs are finite; a program needn't handle non-finite values.
Results may differ from a plain program's by a relative error of at most 0.0003.
Values sent between devices are 32-bit elements; how exact they have to be, the bound alone decides.
A program may use at most 64 MiB of HBM per device.

v0:
```python
import math

import jax
import jax.numpy as jnp
from jax import lax
from jax.sharding import PartitionSpec as P

PART_DEV = 512
SIDE_CELLS = 256
SPAN_CELLS = 1024
SUBREGIONS = 8
S_BINS = 30
MU_BINS = 20


def padded(block, sides, width):
    for axis, dim in sides:
        count = lax.axis_size(axis)
        forward = [(i, i + 1) for i in range(count - 1)]
        backward = [(target, source) for source, target in forward]
        low = lax.ppermute(
            lax.slice_in_dim(block, block.shape[dim] - width, None, axis=dim), axis, forward
        )
        high = lax.ppermute(lax.slice_in_dim(block, 0, width, axis=dim), axis, backward)
        block = jnp.concatenate([low, block, high], axis=dim)
    return block


def from_everyone(x, axis):
    copies = jnp.broadcast_to(x, (lax.axis_size(axis), *x.shape))
    return lax.all_to_all(copies, axis, split_axis=0, concat_axis=0, tiled=True)


def over_copies(x, axis):
    everything = from_everyone(x, axis)
    return jnp.sum(everything, axis=0)


def edge_values():
    return [int(4.0 * 10.0 ** (4.0 * level / S_BINS) + 0.5) for level in range(S_BINS + 1)]


def bin_scale(patches):
    edges = edge_values()
    factor = SIDE_CELLS * SIDE_CELLS * SPAN_CELLS / (patches * PART_DEV * PART_DEV)
    values = []
    for level in range(S_BINS):
        volume = 4.0 * math.pi / 3.0 * (edges[level + 1] ** 1.5 - edges[level] ** 1.5) / MU_BINS
        values = values + [factor / volume] * MU_BINS
    return jnp.asarray(values, dtype=jnp.float32)


def pair_block(own_pos, far_pos, far_weight):
    edges = edge_values()
    radial_gap = jnp.minimum(jnp.abs(own_pos[0][:, None] - far_pos[0][None, :]), 255)
    across_gap = jnp.minimum(jnp.abs(own_pos[1][:, None] - far_pos[1][None, :]), 255)
    depth_gap = jnp.minimum(jnp.abs(own_pos[2][:, None] - far_pos[2][None, :]), 255)
    squared = radial_gap * radial_gap + across_gap * across_gap + depth_gap * depth_gap
    radial_sq = radial_gap * radial_gap * (MU_BINS * MU_BINS)
    s_index = jnp.zeros_like(squared)
    for level in range(1, S_BINS):
        s_index = s_index + (squared >= edges[level]).astype(jnp.int32)
    mu_index = jnp.zeros_like(squared)
    for level in range(1, MU_BINS):
        mu_index = mu_index + (radial_sq >= level * level * squared).astype(jnp.int32)
    inside = (squared >= edges[0]) & (squared < edges[S_BINS])
    s_levels = lax.iota(jnp.int32, S_BINS)
    mu_levels = lax.iota(jnp.int32, MU_BINS)
    s_hot = ((s_index[:, :, None] == s_levels[None, None, :]) & inside[:, :, None]).astype(
        jnp.float32
    )
    s_weighted = (s_hot * far_weight[None, :, None]).astype(jnp.bfloat16)
    mu_hot = (mu_index[:, :, None] == mu_levels[None, None, :]).astype(jnp.bfloat16)
    return jnp.einsum("ijs,ijm->ism", s_weighted, mu_hot, preferred_element_type=jnp.float32)


def local(coords, weights, live):
    live_count = live[0, 0]
    parts = coords.shape[3]
    slots = lax.iota(jnp.int32, parts)
    own_weight = jnp.where(slots < live_count, weights[0, 0].astype(jnp.float32), 0.0)
    own_pos = coords.reshape(3, parts)
    packed = jnp.concatenate(
        [coords.astype(jnp.float32), own_weight.reshape(1, 1, 1, parts)], axis=0
    )
    tile_rows = min(256, parts)
    tiles_live = (live_count + tile_rows - 1) // tile_rows
    empty = jnp.zeros((SUBREGIONS, S_BINS, MU_BINS), jnp.float32)
    region_levels = lax.iota(jnp.int32, SUBREGIONS)
    result = padded(packed, (("shell", 1), ("sky", 2)), 1)
    far_pos = result[:3].reshape(3, 9 * parts).astype(jnp.int32)
    far_weight = result[3].reshape(9 * parts)
    blocks = far_pos.shape[1] // parts

    def add_tile(index, running):
        start = index * tile_rows
        rows_pos = lax.dynamic_slice_in_dim(own_pos, start, tile_rows, 1)
        rows_weight = lax.dynamic_slice_in_dim(own_weight, start, tile_rows, 0)

        def add_block(block, per_row):
            offset = block * parts
            block_pos = lax.dynamic_slice_in_dim(far_pos, offset, parts, 1)
            block_weight = lax.dynamic_slice_in_dim(far_weight, offset, parts, 0)
            return per_row + pair_block(rows_pos, block_pos, block_weight)

        per_row = lax.fori_loop(
            0, blocks, add_block, jnp.zeros((tile_rows, S_BINS, MU_BINS), jnp.float32)
        )
        region = rows_pos[2] // (SPAN_CELLS // SUBREGIONS)
        region_weight = jnp.where(
            region[:, None] == region_levels[None, :], rows_weight[:, None], 0.0
        )
        folded = jnp.sum(region_weight[:, :, None, None] * per_row[:, None, :, :], axis=0)
        return running + folded

    histogram = lax.fori_loop(0, tiles_live, add_tile, empty)
    by_region = histogram.reshape(SUBREGIONS, S_BINS * MU_BINS)
    shell_total = over_copies(jnp.sum(by_region, axis=0), "sky")
    scale = bin_scale(lax.axis_size("sky"))
    leave = (shell_total[None, :] - by_region) * scale[None, :]
    return leave.reshape(1, SUBREGIONS, S_BINS * MU_BINS)


def solution(mesh):
    in_specs = (P(None, "shell", "sky", None), P("shell", "sky", None), P("shell", "sky"))
    out_specs = P("shell", "sky", None)
    return jax.shard_map(local, mesh=mesh, in_specs=in_specs, out_specs=out_specs, check_vma=False)
```

profile of v0, /device:TPU:2, one launch (start us, length us, event | category | flops | bytes accessed | tf_op | source)
XLA Modules:
  0.0 247.7 jit_solution(7362218877141523482)
XLA Ops:
  7.9 3.2 %collective-permute-done = f32[4,1,1,512]{3,2,1,0:T(1,128)S(1)} collective-permute-done((f32[4,1,1,512]{3,2,1,0:T(1,128)S(1)}, f32[4,1,1,512]{3,2,1,0:T(1,128)S(1)}, u32[]{:S(2)}, u32[]{:S(2)}) %collective-permute-start) | collective-permute-done | bytes 8224 | tf_op jit(solution)/shard_map/ppermute | solution.py:21
  12.5 5.8 %collective-permute-start.2 = (f32[4,3,1,512]{3,2,1,0:T(1,128)S(1)}, f32[4,3,1,512]{3,2,1,0:T(1,128)S(1)}, u32[]{:S(2)}, u32[]{:S(2)}) collective-permute-start(f32[4,3,1,512]{3,2,1,0:T(1,128)S(1)} %pad_maximum_fusion.2), channel_id=1, source_target_pairs={{0,1},{1,2},{2,3},{3,4},{4,5},{5,6},{6,7},{7,8},{8,9},{9,10},{10,1... | collective-permute-start | bytes 73736 | tf_op jit(solution)/shard_map/ppermute | solution.py:21
  20.1 102.0 %while.36 = (s32[]{:T(128)}, f32[8,30,20]{0,2,1:T(8,128)S(1)}, s32[]{:T(128)}, s32[3,512]{1,0:T(4,128)S(1)}, f32[512]{0:T(512)S(1)}, /*index=5*/s32[3,4608]{1,0:...) while((s32[]{:T(128)}, f32[8,30,20]{0,2,1:T(8,128)S(1)}, ...), condition=%wide.region_4.5_spmd.clone, body=%wide.region_0.4_spmd.clone.sunk | while | flops 199642880 | bytes 5579304 | solution.py:116
  20.1 98.6 %while.37 = (s32[]{:T(128)}, f32[256,30,20]{1,2,0:T(8,128)}, s32[3,256]{1,0:T(4,128)S(1)}, s32[3,4608]{1,0:T(4,128)S(1)}, bf16[4608]{0:T(1024)(128)(2,1)S(1)}, /...) while((s32[]{:T(128)}, f32[256,30,20]{1,2,0:T(8,128)}, ...), condition=%wide.region_2.2_spmd.clone, body=%wide.region_1.1_spmd.clone.sunk | while | flops 197177344 | bytes 3628245 | solution.py:106
  20.2 3.3 %convert_add_fusion.3 = (s32[256,512]{1,0:T(8,128)S(1)}, s32[256,512]{1,0:T(8,128)S(1)}) fusion(s32[512]{0:T(512)S(1)} %bitcast.35, s32[256]{0:T(256)S(1)} %bitcast.39, s32[512]{0:T(512)S(1)} %bitcast.31, s32[256]{0:T(256)S(1)} %bitcast.37, s32[512]{0:T(512)S(1)} %bitcast.33, s32[256]{0:T(256)S(1)} %bitcast.41), kind=kLoop, calls=%fused_computation.31.clone.1 | loop fusion | flops 22937600 | bytes 1057792 | tf_op jit(solution)/shard_map/while/body/while/body/eval_jaxpr/add | solution.py:62
  24.1 5.7 %select_add_fusion.2 = f32[256,30,20]{1,2,0:T(8,128)} fusion(f32[256,30,20]{1,2,0:T(8,128)} %get-tuple-element.400, s32[256,512]{1,0:T(8,128)S(1)} %get-tuple-element.386, bf16[512]{0:T(512)(128)(2,1)S(1)} %dynamic_slice.36, s32[256,512]{1,0:T(8,128)S(1)} %get-tuple-element.387, pred[256,512]{1,0:T(8,128)(4,1)S(1)} %compare_and_fusion.2, ...), kind=kOutput, calls=%fused_computation.11.clone.1 | convolution fusion | flops 172011520 | bytes 2409473 | tf_op jit(solution)/shard_map/while/body/while/body/eval_jaxpr/ijs,ijm->ism/dot_general | solution.py:74
  30.0 3.3 %convert_add_fusion.3 = (s32[256,512]{1,0:T(8,128)S(1)}, s32[256,512]{1,0:T(8,128)S(1)}) fusion(s32[512]{0:T(512)S(1)} %bitcast.35, s32[256]{0:T(256)S(1)} %bitcast.39, s32[512]{0:T(512)S(1)} %bitcast.31, s32[256]{0:T(256)S(1)} %bitcast.37, s32[512]{0:T(512)S(1)} %bitcast.33, s32[256]{0:T(256)S(1)} %bitcast.41), kind=kLoop, calls=%fused_computation.31.clone.1 | loop fusion | flops 22937600 | bytes 1057792 | tf_op jit(solution)/shard_map/while/body/while/body/eval_jaxpr/add | solution.py:62
  33.9 7.1 %select_add_fusion.2 = f32[256,30,20]{1,2,0:T(8,128)} fusion(f32[256,30,20]{1,2,0:T(8,128)} %get-tuple-element.400, s32[256,512]{1,0:T(8,128)S(1)} %get-tuple-element.386, bf16[512]{0:T(512)(128)(2,1)S(1)} %dynamic_slice.36, s32[256,512]{1,0:T(8,128)S(1)} %get-tuple-element.387, pred[256,512]{1,0:T(8,128)(4,1)S(1)} %compare_and_fusion.2, ...), kind=kOutput, calls=%fused_computation.11.clone.1 | convolution fusion | flops 172011520 | bytes 2409473 | tf_op jit(solution)/shard_map/while/body/while/body/eval_jaxpr/ijs,ijm->ism/dot_general | solution.py:74
  41.1 3.3 %convert_add_fusion.3 = (s32[256,512]{1,0:T(8,128)S(1)}, s32[256,512]{1,0:T(8,128)S(1)}) fusion(s32[512]{0:T(512)S(1)} %bitcast.35, s32[256]{0:T(256)S(1)} %bitcast.39, s32[512]{0:T(512)S(1)} %bitcast.31, s32[256]{0:T(256)S(1)} %bitcast.37, s32[512]{0:T(512)S(1)} %bitcast.33, s32[256]{0:T(256)S(1)} %bitcast.41), kind=kLoop, calls=%fused_computation.31.clone.1 | loop fusion | flops 22937600 | bytes 1057792 | tf_op jit(solution)/shard_map/while/body/while/body/eval_jaxpr/add | solution.py:62
  45.0 7.1 %select_add_fusion.2 = f32[256,30,20]{1,2,0:T(8,128)} fusion(f32[256,30,20]{1,2,0:T(8,128)} %get-tuple-element.400, s32[256,512]{1,0:T(8,128)S(1)} %get-tuple-element.386, bf16[512]{0:T(512)(128)(2,1)S(1)} %dynamic_slice.36, s32[256,512]{1,0:T(8,128)S(1)} %get-tuple-element.387, pred[256,512]{1,0:T(8,128)(4,1)S(1)} %compare_and_fusion.2, ...), kind=kOutput, calls=%fused_computation.11.clone.1 | convolution fusion | flops 172011520 | bytes 2409473 | tf_op jit(solution)/shard_map/while/body/while/body/eval_jaxpr/ijs,ijm->ism/dot_general | solution.py:74
  52.2 3.3 %convert_add_fusion.3 = (s32[256,512]{1,0:T(8,128)S(1)}, s32[256,512]{1,0:T(8,128)S(1)}) fusion(s32[512]{0:T(512)S(1)} %bitcast.35, s32[256]{0:T(256)S(1)} %bitcast.39, s32[512]{0:T(512)S(1)} %bitcast.31, s32[256]{0:T(256)S(1)} %bitcast.37, s32[512]{0:T(512)S(1)} %bitcast.33, s32[256]{0:T(256)S(1)} %bitcast.41), kind=kLoop, calls=%fused_computation.31.clone.1 | loop fusion | flops 22937600 | bytes 1057792 | tf_op jit(solution)/shard_map/while/body/while/body/eval_jaxpr/add | solution.py:62
  56.1 7.1 %select_add_fusion.2 = f32[256,30,20]{1,2,0:T(8,128)} fusion(f32[256,30,20]{1,2,0:T(8,128)} %get-tuple-element.400, s32[256,512]{1,0:T(8,128)S(1)} %get-tuple-element.386, bf16[512]{0:T(512)(128)(2,1)S(1)} %dynamic_slice.36, s32[256,512]{1,0:T(8,128)S(1)} %get-tuple-element.387, pred[256,512]{1,0:T(8,128)(4,1)S(1)} %compare_and_fusion.2, ...), kind=kOutput, calls=%fused_computation.11.clone.1 | convolution fusion | flops 172011520 | bytes 2409473 | tf_op jit(solution)/shard_map/while/body/while/body/eval_jaxpr/ijs,ijm->ism/dot_general | solution.py:74
  63.3 3.3 %convert_add_fusion.3 = (s32[256,512]{1,0:T(8,128)S(1)}, s32[256,512]{1,0:T(8,128)S(1)}) fusion(s32[512]{0:T(512)S(1)} %bitcast.35, s32[256]{0:T(256)S(1)} %bitcast.39, s32[512]{0:T(512)S(1)} %bitcast.31, s32[256]{0:T(256)S(1)} %bitcast.37, s32[512]{0:T(512)S(1)} %bitcast.33, s32[256]{0:T(256)S(1)} %bitcast.41), kind=kLoop, calls=%fused_computation.31.clone.1 | loop fusion | flops 22937600 | bytes 1057792 | tf_op jit(solution)/shard_map/while/body/while/body/eval_jaxpr/add | solution.py:62
  67.2 7.1 %select_add_fusion.2 = f32[256,30,20]{1,2,0:T(8,128)} fusion(f32[256,30,20]{1,2,0:T(8,128)} %get-tuple-element.400, s32[256,512]{1,0:T(8,128)S(1)} %get-tuple-element.386, bf16[512]{0:T(512)(128)(2,1)S(1)} %dynamic_slice.36, s32[256,512]{1,0:T(8,128)S(1)} %get-tuple-element.387, pred[256,512]{1,0:T(8,128)(4,1)S(1)} %compare_and_fusion.2, ...), kind=kOutput, calls=%fused_computation.11.clone.1 | convolution fusion | flops 172011520 | bytes 2409473 | tf_op jit(solution)/shard_map/while/body/while/body/eval_jaxpr/ijs,ijm->ism/dot_general | solution.py:74
  74.4 3.3 %convert_add_fusion.3 = (s32[256,512]{1,0:T(8,128)S(1)}, s32[256,512]{1,0:T(8,128)S(1)}) fusion(s32[512]{0:T(512)S(1)} %bitcast.35, s32[256]{0:T(256)S(1)} %bitcast.39, s32[512]{0:T(512)S(1)} %bitcast.31, s32[256]{0:T(256)S(1)} %bitcast.37, s32[512]{0:T(512)S(1)} %bitcast.33, s32[256]{0:T(256)S(1)} %bitcast.41), kind=kLoop, calls=%fused_computation.31.clone.1 | loop fusion | flops 22937600 | bytes 1057792 | tf_op jit(solution)/shard_map/while/body/while/body/eval_jaxpr/add | solution.py:62
  78.3 7.1 %select_add_fusion.2 = f32[256,30,20]{1,2,0:T(8,128)} fusion(f32[256,30,20]{1,2,0:T(8,128)} %get-tuple-element.400, s32[256,512]{1,0:T(8,128)S(1)} %get-tuple-element.386, bf16[512]{0:T(512)(128)(2,1)S(1)} %dynamic_slice.36, s32[256,512]{1,0:T(8,128)S(1)} %get-tuple-element.387, pred[256,512]{1,0:T(8,128)(4,1)S(1)} %compare_and_fusion.2, ...), kind=kOutput, calls=%fused_computation.11.clone.1 | convolution fusion | flops 172011520 | bytes 2409473 | tf_op jit(solution)/shard_map/while/body/while/body/eval_jaxpr/ijs,ijm->ism/dot_general | solution.py:74
  85.5 3.3 %convert_add_fusion.3 = (s32[256,512]{1,0:T(8,128)S(1)}, s32[256,512]{1,0:T(8,128)S(1)}) fusion(s32[512]{0:T(512)S(1)} %bitcast.35, s32[256]{0:T(256)S(1)} %bitcast.39, s32[512]{0:T(512)S(1)} %bitcast.31, s32[256]{0:T(256)S(1)} %bitcast.37, s32[512]{0:T(512)S(1)} %bitcast.33, s32[256]{0:T(256)S(1)} %bitcast.41), kind=kLoop, calls=%fused_computation.31.clone.1 | loop fusion | flops 22937600 | bytes 1057792 | tf_op jit(solution)/shard_map/while/body/while/body/eval_jaxpr/add | solution.py:62
  89.4 7.1 %select_add_fusion.2 = f32[256,30,20]{1,2,0:T(8,128)} fusion(f32[256,30,20]{1,2,0:T(8,128)} %get-tuple-element.400, s32[256,512]{1,0:T(8,128)S(1)} %get-tuple-element.386, bf16[512]{0:T(512)(128)(2,1)S(1)} %dynamic_slice.36, s32[256,512]{1,0:T(8,128)S(1)} %get-tuple-element.387, pred[256,512]{1,0:T(8,128)(4,1)S(1)} %compare_and_fusion.2, ...), kind=kOutput, calls=%fused_computation.11.clone.1 | convolution fusion | flops 172011520 | bytes 2409473 | tf_op jit(solution)/shard_map/while/body/while/body/eval_jaxpr/ijs,ijm->ism/dot_general | solution.py:74
  96.6 3.3 %convert_add_fusion.3 = (s32[256,512]{1,0:T(8,128)S(1)}, s32[256,512]{1,0:T(8,128)S(1)}) fusion(s32[512]{0:T(512)S(1)} %bitcast.35, s32[256]{0:T(256)S(1)} %bitcast.39, s32[512]{0:T(512)S(1)} %bitcast.31, s32[256]{0:T(256)S(1)} %bitcast.37, s32[512]{0:T(512)S(1)} %bitcast.33, s32[256]{0:T(256)S(1)} %bitcast.41), kind=kLoop, calls=%fused_computation.31.clone.1 | loop fusion | flops 22937600 | bytes 1057792 | tf_op jit(solution)/shard_map/while/body/while/body/eval_jaxpr/add | solution.py:62
  100.5 7.1 %select_add_fusion.2 = f32[256,30,20]{1,2,0:T(8,128)} fusion(f32[256,30,20]{1,2,0:T(8,128)} %get-tuple-element.400, s32[256,512]{1,0:T(8,128)S(1)} %get-tuple-element.386, bf16[512]{0:T(512)(128)(2,1)S(1)} %dynamic_slice.36, s32[256,512]{1,0:T(8,128)S(1)} %get-tuple-element.387, pred[256,512]{1,0:T(8,128)(4,1)S(1)} %compare_and_fusion.2, ...), kind=kOutput, calls=%fused_computation.11.clone.1 | convolution fusion | flops 172011520 | bytes 2409473 | tf_op jit(solution)/shard_map/while/body/while/body/eval_jaxpr/ijs,ijm->ism/dot_general | solution.py:74
  107.7 3.3 %convert_add_fusion.3 = (s32[256,512]{1,0:T(8,128)S(1)}, s32[256,512]{1,0:T(8,128)S(1)}) fusion(s32[512]{0:T(512)S(1)} %bitcast.35, s32[256]{0:T(256)S(1)} %bitcast.39, s32[512]{0:T(512)S(1)} %bitcast.31, s32[256]{0:T(256)S(1)} %bitcast.37, s32[512]{0:T(512)S(1)} %bitcast.33, s32[256]{0:T(256)S(1)} %bitcast.41), kind=kLoop, calls=%fused_computation.31.clone.1 | loop fusion | flops 22937600 | bytes 1057792 | tf_op jit(solution)/shard_map/while/body/while/body/eval_jaxpr/add | solution.py:62
  111.6 7.1 %select_add_fusion.2 = f32[256,30,20]{1,2,0:T(8,128)} fusion(f32[256,30,20]{1,2,0:T(8,128)} %get-tuple-element.400, s32[256,512]{1,0:T(8,128)S(1)} %get-tuple-element.386, bf16[512]{0:T(512)(128)(2,1)S(1)} %dynamic_slice.36, s32[256,512]{1,0:T(8,128)S(1)} %get-tuple-element.387, pred[256,512]{1,0:T(8,128)(4,1)S(1)} %compare_and_fusion.2, ...), kind=kOutput, calls=%fused_computation.11.clone.1 | convolution fusion | flops 172011520 | bytes 2409473 | tf_op jit(solution)/shard_map/while/body/while/body/eval_jaxpr/ijs,ijm->ism/dot_general | solution.py:74
  123.0 114.0 %all-to-all-start = ((f32[16,1,600]{2,1,0:T(1,128)}), f32[16,1,600]{2,1,0:T(1,128)S(1)}, u32[]{:S(2)}, u32[]{:S(2)}) async-start(f32[16,1,600]{2,1,0:T(1,128)} %broadcast_in_dim.55), calls=%async_computation | async-start | bytes 81920 | tf_op jit(solution)/shard_map/all_to_all | solution.py:31
  237.4 9.6 %all-to-all-done = f32[16,1,600]{2,1,0:T(1,128)S(1)} async-done(((f32[16,1,600]{2,1,0:T(1,128)}), f32[16,1,600]{2,1,0:T(1,128)S(1)}, u32[]{:S(2)}, u32[]{:S(2)}) %all-to-all-start) | async-done | bytes 38432 | tf_op jit(solution)/shard_map/all_to_all | solution.py:31
  (73 shorter events, 22.1 us)
Async XLA Ops:
  2.1 5.9 %collective-permute-start.1 = (f32[4,1,1,512]{3,2,1,0:T(1,128)S(1)}, f32[4,1,1,512]{3,2,1,0:T(1,128)S(1)}, u32[]{:S(2)}, u32[]{:S(2)}) collective-permute-start(f32[4,1,1,512]{3,2,1,0:T(1,128)S(1)} %pad_maximum_fusion.3), channel_id=1, source_target_pairs={{16,0},{32,16},{48,32},{64,48},{80,64},{96,80},{112,96},{128,112},... | collective-permute-start | bytes 24584 | tf_op jit(solution)/shard_map/ppermute | solution.py:24
  5.3 5.9 %collective-permute-start = (f32[4,1,1,512]{3,2,1,0:T(1,128)S(1)}, f32[4,1,1,512]{3,2,1,0:T(1,128)S(1)}, u32[]{:S(2)}, u32[]{:S(2)}) collective-permute-start(f32[4,1,1,512]{3,2,1,0:T(1,128)S(1)} %pad_maximum_fusion.3), channel_id=1, source_target_pairs={{0,16},{16,32},{32,48},{48,64},{64,80},{80,96},{96,112},{112,128},... | collective-permute-start | bytes 24584 | tf_op jit(solution)/shard_map/ppermute | solution.py:21
  11.2 7.8 %collective-permute-start.3 = (f32[4,3,1,512]{3,2,1,0:T(1,128)S(1)}, f32[4,3,1,512]{3,2,1,0:T(1,128)S(1)}, u32[]{:S(2)}, u32[]{:S(2)}) collective-permute-start(f32[4,3,1,512]{3,2,1,0:T(1,128)S(1)} %pad_maximum_fusion.2), channel_id=1, source_target_pairs={{1,0},{2,1},{3,2},{4,3},{5,4},{6,5},{7,6},{8,7},{9,8},{10,9},{11,1... | collective-permute-start | bytes 73736 | tf_op jit(solution)/shard_map/ppermute | solution.py:24
  12.5 7.3 %collective-permute-start.2 = (f32[4,3,1,512]{3,2,1,0:T(1,128)S(1)}, f32[4,3,1,512]{3,2,1,0:T(1,128)S(1)}, u32[]{:S(2)}, u32[]{:S(2)}) collective-permute-start(f32[4,3,1,512]{3,2,1,0:T(1,128)S(1)} %pad_maximum_fusion.2), channel_id=1, source_target_pairs={{0,1},{1,2},{2,3},{3,4},{4,5},{5,6},{6,7},{7,8},{8,9},{9,10},{10,1... | collective-permute-start | bytes 73736 | tf_op jit(solution)/shard_map/ppermute | solution.py:21
  20.1 227.0 %copy-start = (f32[600]{0:T(1024)S(1)}, f32[600]{0:T(1024)}, u32[]{:S(2)}) copy-start(f32[600]{0:T(1024)} %constant.397.clone) | copy-start | bytes 7204
  123.0 124.0 %all-to-all-start = ((f32[16,1,600]{2,1,0:T(1,128)}), f32[16,1,600]{2,1,0:T(1,128)S(1)}, u32[]{:S(2)}, u32[]{:S(2)}) async-start(f32[16,1,600]{2,1,0:T(1,128)} %broadcast_in_dim.55), calls=%async_computation | async-start | bytes 81920 | tf_op jit(solution)/shard_map/all_to_all | solution.py:31
where the time goes:
time: 248 us
  starting transfers between devices  126 us (51%)
  matrix products  62.5 us (25%)
  other arithmetic  38.2 us (15%)
  waiting for transfers between devices  13.7 us (6%)
  local copies, waits for them, and re-layouts  5.97 us (2%)
    all_to_all x1, starting transfers between devices, from_everyone(): return lax.all_to_all(copies, axis, split_axis=0, concat_axis=0, tiled=True)  114 us
    dot_general x9, matrix products, pair_block(): jnp.einsum('ijs,ijm->ism', s_weighted, mu_hot, preferred_element_type=jnp...  62.5 us
    add x9, other arithmetic, pair_block(): s_index = s_index + (squared >= edges[level]).astype(jnp.int32)  29.3 us
    all_to_all x1, waiting for transfers between devices, from_everyone(): return lax.all_to_all(copies, axis, split_axis=0, concat_axis=0, tiled=True)  9.64 us
    ppermute x2, starting transfers between devices, padded(): lax.ppermute(lax.slice_in_dim(block, block.shape[dim] - width, None, axis...  7.73 us
    and x9, other arithmetic, pair_block(): inside = (squared >= edges[0]) & (squared < edges[S_BINS])  5.04 us
  transfers between devices with their start and end apart: 5, of which 3 were waited for; matrix products, arithmetic and copies ran while one was open for 1% of the time, Pallas kernels for 0%

commit v1 on v0

v1 whole, which is shorter than its diff:
```python
import functools, math
import jax, jax.numpy as jnp
from jax import lax
from jax.experimental import pallas as pl
from jax.experimental.pallas import tpu as pltpu
from jax.sharding import PartitionSpec as P

PART_DEV = 512
SIDE_CELLS = 256
SPAN_CELLS = 1024
SUBREGIONS = 8
S_BINS = 30
MU_BINS = 20
REACH = 199
GROUPS = 24
STEP = 16
ROWS = PART_DEV // STEP
DIRS = tuple((da, db) for da in (-1, 0, 1) for db in (-1, 0, 1) if (da, db) != (0, 0))
F32 = jnp.float32
BF16 = jnp.bfloat16


def sort_kernel(live_ref, coords_ref, weight_ref, lists_ref, own_ref, start_ref):
    def body(acc0, acc1, acc2, acc3, tall0, tall1):
        for acc in (acc0, acc1, acc2, acc3, tall0, tall1):
            pltpu.matmul_pop(acc)
        n = PART_DEV
        x = (coords_ref[0:1, :] & (SIDE_CELLS - 1)).astype(F32)
        y = (coords_ref[1:2, :] & (SIDE_CELLS - 1)).astype(F32)
        zi = coords_ref[2:3, :]
        region = zi >> 7
        z_high = region.astype(F32)
        z_low = (zi & 127).astype(F32)
        slot = lax.broadcasted_iota(jnp.int32, (1, n), 1)
        alive = slot < live_ref[0, 0]
        w = jnp.where(alive, weight_ref[0:1, :].astype(F32), 0.0)
        key = (jnp.where(alive, zi * n, SPAN_CELLS * n) + slot).astype(F32)
        key_column = jnp.transpose(jnp.broadcast_to(key, (128, n)))[:, 0:1]
        before = jnp.where(key_column < key, 1.0, 0.0).astype(BF16)
        valid = []
        for da, db in DIRS:
            ok = alive
            if da > 0:
                ok = ok & (x >= SIDE_CELLS - REACH)
            if da < 0:
                ok = ok & (x <= REACH - 1)
            if db > 0:
                ok = ok & (y >= SIDE_CELLS - REACH)
            if db < 0:
                ok = ok & (y <= REACH - 1)
            valid.append(ok)
        valid.append(alive)
        ones = [jnp.where(ok, 1.0, 0.0) for ok in valid]
        flags = jnp.concatenate(ones + [jnp.zeros((7, n), F32)], axis=0).astype(BF16)
        for half in range(2):
            rows = slice(256 * half, 256 * half + 256)
            pltpu.matmul_push_rhs(before[rows, 0:256], staging_register=0, mxu_index=0)
            pltpu.matmul_acc_lhs(acc0, flags[:, rows], load_staged_rhs=0)
            pltpu.matmul_push_rhs(before[rows, 256:512], staging_register=0, mxu_index=1)
            pltpu.matmul_acc_lhs(acc1, flags[:, rows], load_staged_rhs=0)
        rank = jnp.concatenate([pltpu.matmul_pop(acc0), pltpu.matmul_pop(acc1)], axis=1)
        attrs = jnp.concatenate([x, y, z_high, z_low, w, jnp.zeros((11, n), F32)], axis=0).astype(BF16)
        place = lax.broadcasted_iota(jnp.int32, (n, 1), 0).astype(F32)
        accs = ((acc0, acc1), (acc2, acc3))
        for d in range(9):
            target = jnp.where(valid[d], rank[d : d + 1, :], -1.0)
            hot = jnp.where(place == target, 1.0, 0.0).astype(BF16)
            pair = accs[d % 2]
            for half in range(2):
                cols = slice(256 * half, 256 * half + 256)
                for mxu in range(2):
                    pltpu.matmul_push_rhs(hot[256 * mxu : 256 * mxu + 256, cols], staging_register=0, mxu_index=mxu, transpose=True)
                    pltpu.matmul_acc_lhs(pair[mxu], attrs[:, cols], load_staged_rhs=0)
            da, db = DIRS[d] if d < 8 else (0, 0)
            for mxu in range(2):
                got = pltpu.matmul_pop(pair[mxu])
                lanes = slice(256 * mxu, 256 * mxu + 256)
                lists_ref[d, 0:1, lanes] = got[0:1] - float(SIDE_CELLS * da)
                lists_ref[d, 1:2, lanes] = got[1:2] - float(SIDE_CELLS * db)
                lists_ref[d, 2:3, lanes] = got[2:3] * 128.0 + got[3:4]
                lists_ref[d, 3:4, lanes] = got[4:5]
        shift = jnp.zeros((1, n), F32)
        first = jnp.zeros((1, 1), F32)
        group = jnp.zeros((1, 1), F32)
        starts = []
        for r in range(SUBREGIONS):
            here = alive & (region == r)
            starts.append(group)
            shift = jnp.where(here, 32.0 * group - first, shift)
            count = jnp.sum(jnp.where(here, 1.0, 0.0), axis=1, keepdims=True)
            first = first + count
            group = group + jnp.floor((count + 31.0) * (1.0 / 32.0))
        starts = starts + [group]
        row = lax.broadcasted_iota(jnp.int32, (8, 128), 1)
        table = jnp.zeros((8, 128), F32)
        for r in range(9):
            table = jnp.where(row == r, starts[r], table)
        start_ref[...] = table.astype(jnp.int32)
        target = jnp.where(alive, rank[8:9, :] + shift, -1.0)
        wide = lax.broadcasted_iota(jnp.int32, (GROUPS * 32, 1), 0).astype(F32)
        hot = jnp.where(wide == target, 1.0, 0.0).astype(BF16)
        rhs = jnp.concatenate([attrs, jnp.zeros((240, n), BF16)], axis=0)
        half_rows = GROUPS * 16
        for half in range(2):
            cols = slice(256 * half, 256 * half + 256)
            for mxu, acc in ((0, tall0), (1, tall1)):
                pltpu.matmul_push_rhs(rhs[:, cols], staging_register=0, mxu_index=mxu, transpose=True)
                pltpu.matmul_acc_lhs(acc, hot[half_rows * mxu : half_rows * mxu + half_rows, cols], load_staged_rhs=0)
        lane = lax.broadcasted_iota(jnp.int32, (8, 128), 1) // 32
        for mxu, acc in ((0, tall0), (1, tall1)):
            got = pltpu.matmul_pop(acc)[:, 0:128]
            for g in range(GROUPS // 2):
                parts = []
                for q in range(4):
                    block = got[32 * g + 8 * q : 32 * g + 8 * q + 8]
                    deep = block[:, 2:3] * 128.0 + block[:, 3:4]
                    parts.append([jnp.broadcast_to(v, (8, 128)) for v in (block[:, 0:1], block[:, 1:2], deep, block[:, 4:5])])
                for k in range(4):
                    value = parts[0][k]
                    for q in range(1, 4):
                        value = jnp.where(lane == q, parts[q][k], value)
                    own_ref[k, mxu * (GROUPS // 2) + g] = value

    pl.run_scoped(
        body,
        pltpu.ACC(0)((16, 256), F32),
        pltpu.ACC(1)((16, 256), F32),
        pltpu.ACC(0)((16, 256), F32),
        pltpu.ACC(1)((16, 256), F32),
        pltpu.ACC(0)((GROUPS * 16, 256), F32),
        pltpu.ACC(1)((GROUPS * 16, 256), F32),
    )


def sort_call(coords, weights, live):
    return pl.pallas_call(
        sort_kernel,
        out_shape=(
            jax.ShapeDtypeStruct((9, 4, PART_DEV), F32),
            jax.ShapeDtypeStruct((4, GROUPS, 8, 128), F32),
            jax.ShapeDtypeStruct((8, 128), jnp.int32),
        ),
        in_specs=[
            pl.BlockSpec(memory_space=pltpu.SMEM),
            pl.BlockSpec(memory_space=pltpu.VMEM),
            pl.BlockSpec(memory_space=pltpu.VMEM),
        ],
        out_specs=[pl.BlockSpec(memory_space=pltpu.VMEM)] * 3,
    )(live, coords, weights)


LOG_SCALE = (S_BINS / 4.0) / math.log2(10.0)
LOG_BASE = -4.515457845
LEVELS_U = 24
LEVELS_V = 25
TILES = 4
V_ROWS = 208
DUMMY = 9 * ROWS


def count_kernel(start_ref, lists_ref, got_ref, own_ref, out_ref, rows_ref, table_ref, table_sm, hot_u, hot_v, sem):
    def body(a0, a1, b0, b1):
        sets = ((a0, a1), (b0, b1))
        for acc in (a0, a1, b0, b1):
            pltpu.matmul_pop(acc)
        zs, ws = own_ref[2], own_ref[3]
        z_min = jnp.min(jnp.min(jnp.where(ws > 0.0, zs, 1e6), axis=1), axis=1, keepdims=True)
        z_max = jnp.max(jnp.max(jnp.where(ws > 0.0, zs, -1e6), axis=1), axis=1, keepdims=True)
        lane = lax.broadcasted_iota(jnp.int32, (GROUPS, 256), 1).astype(F32)
        table = jnp.full((GROUPS, 256), float(DUMMY), F32)
        total = jnp.zeros((GROUPS, 1), F32)
        for d in range(9):
            src = lists_ref.at[8] if d == 8 else got_ref.at[d]
            z_row = jnp.where(src[3:4, :] > 0.0, src[2:3, :], 2e6)
            low = jnp.sum(jnp.where(z_row < z_min - float(REACH), 1.0, 0.0), axis=1, keepdims=True)
            high = jnp.sum(jnp.where(z_row <= z_max + float(REACH), 1.0, 0.0), axis=1, keepdims=True)
            first = jnp.floor(low * (1.0 / STEP))
            count = jnp.where(high > low, jnp.floor((high - STEP * first + 31.0) * (1.0 / 32.0)), 0.0)
            at = lane - total
            table = jnp.where((at >= 0.0) & (at < count), at * 2.0 + (first + float(ROWS * d)), table)
            total = total + count
        batches = jnp.floor((total + (TILES - 1.0)) * (1.0 / TILES))
        table = jnp.where(lane == 255.0, batches, table)
        table_ref[0:GROUPS, :] = table.astype(jnp.int32)
        tail = lax.broadcasted_iota(jnp.int32, (8, 256), 1)
        table_ref[GROUPS : GROUPS + 8, :] = jnp.where(tail == 255, 1 << 20, DUMMY)
        copy = pltpu.make_async_copy(table_ref, table_sm, sem)
        copy.start()
        lane = lax.broadcasted_iota(jnp.int32, (8, 128), 1)
        for d in range(9):
            src = lists_ref.at[8] if d == 8 else got_ref.at[d]
            wide = []
            for t in range(4):
                block = src[:, 128 * t : 128 * t + 128]
                block = jnp.concatenate([block, block], axis=0)
                for k in range(4):
                    part = block if k == 0 else pltpu.roll(block, 128 - 32 * k, 1)
                    part = jnp.where(lane < 32, part, pltpu.roll(part, 32, 1))
                    part = jnp.where(lane < 64, part, pltpu.roll(part, 64, 1))
                    wide.append(part)
            turned = [pltpu.roll(part, 16, 1) for part in wide] + [jnp.zeros((8, 128), F32)]
            for k in range(16):
                rows_ref[ROWS * d + 2 * k] = wide[k]
                rows_ref[ROWS * d + 2 * k + 1] = jnp.where((lane & 31) < 16, turned[k], turned[k + 1])
        rows_ref[DUMMY] = jnp.zeros((8, 128), F32)
        for buf in range(2):
            hot_u[buf, 8 * LEVELS_U :, :] = jnp.zeros((256 - 8 * LEVELS_U, 128 * TILES), BF16)
        copy.wait()
        trips = []
        for r in range(SUBREGIONS):
            begin, end = start_ref[0, r], start_ref[0, r + 1]
            number = lax.fori_loop(begin, end, lambda g, n: n + table_sm[g, 255], jnp.int32(0))
            last = jnp.maximum(end - 1, 0)

            @pl.when(number % 2 == 1)
            def _():
                table_sm[last, 255] = table_sm[last, 255] + 1

            trips.append((number + 1) // 2)

        zero = jnp.zeros((16, 128), BF16)

        stop = start_ref[0, SUBREGIONS]

        def fill(state, buf):
            g, b = state
            group = jnp.minimum(g, GROUPS - 1)
            xi, yi, zi, wi = own_ref[0, group], own_ref[1, group], own_ref[2, group], own_ref[3, group]
            w_own = jnp.concatenate([wi, wi], axis=0).astype(BF16)
            for t in range(TILES):
                row = table_sm[g, TILES * b + t]
                dx = xi - rows_ref[row, 0:1, :]
                dy = yi - rows_ref[row, 1:2, :]
                dz = zi - rows_ref[row, 2:3, :]
                w_far = jnp.broadcast_to(rows_ref[row, 3:4, :].astype(BF16), (16, 128))
                dx2 = dx * dx
                q = dx2 + dy * dy + dz * dz
                s = jnp.floor(jnp.log2(q + 0.48) * LOG_SCALE + LOG_BASE)
                near = jnp.floor(jnp.abs(dx) * lax.rsqrt(q) * float(MU_BINS) + 0.5)
                mu = jnp.where(near * near * q > dx2 * float(MU_BINS * MU_BINS), near - 1.0, near)
                c = s * float(MU_BINS) + jnp.minimum(mu, MU_BINS - 1.0)
                u = jnp.floor(c * (1.0 / LEVELS_V) + 0.01)
                v = c - u * float(LEVELS_V)
                u2 = jnp.concatenate([u, u - 1.0], axis=0).astype(BF16)
                v2 = jnp.concatenate([v, v - 1.0], axis=0).astype(BF16)
                lanes = slice(128 * t, 128 * t + 128)
                for k in range(LEVELS_U // 2):
                    hot_u[buf, 16 * k : 16 * k + 16, lanes] = jnp.where(u2 == jnp.bfloat16(2 * k), w_far, zero)
                for k in range(V_ROWS // 16):
                    hot_v[buf, 16 * k : 16 * k + 16, lanes] = jnp.where(v2 == jnp.bfloat16(2 * k), w_own, zero)
            b = b + 1
            over = b >= table_sm[g, 255]
            g = jnp.where(over, g + 1, g)
            g = jnp.where(g >= stop, GROUPS, g)
            return g, jnp.where(over, 0, b)

        def push(buf):
            for mxu in range(2):
                pltpu.matmul_push_rhs(hot_u[buf, :, 256 * mxu : 256 * mxu + 256], staging_register=buf, mxu_index=mxu, transpose=True)

        def multiply(buf, accs):
            for mxu in range(2):
                pltpu.matmul_acc_lhs(accs[mxu], hot_v[buf, :, 256 * mxu : 256 * mxu + 256], load_staged_rhs=buf)

        state = (jnp.where(stop > 0, 0, GROUPS).astype(jnp.int32), jnp.int32(0))
        state = fill(state, 0)
        push(0)
        state = fill(state, 1)
        sub = lax.broadcasted_iota(jnp.int32, (8, 256), 0)
        diagonal = sub == (lax.broadcasted_iota(jnp.int32, (8, 256), 1) & 7)

        def drain(r):
            accs = sets[r % 2]
            both = pltpu.matmul_pop(accs[0]) + pltpu.matmul_pop(accs[1])
            for v in range(V_ROWS // 8):
                out_ref[r, v : v + 1, :] = jnp.sum(jnp.where(diagonal, both[8 * v : 8 * v + 8], 0.0), axis=0, keepdims=True)
            out_ref[r, V_ROWS // 8 :, :] = jnp.zeros((32 - V_ROWS // 8, 256), F32)

        for r in range(SUBREGIONS):
            accs = sets[r % 2]

            def trip(_, state):
                push(1)
                multiply(0, accs)
                state = fill(state, 0)
                push(0)
                multiply(1, accs)
                return fill(state, 1)

            state = lax.fori_loop(0, trips[r], trip, state)
            if r > 0:
                drain(r - 1)
        multiply(0, sets[(SUBREGIONS - 1) % 2])
        drain(SUBREGIONS - 1)

    pl.run_scoped(
        body,
        pltpu.ACC(0)((V_ROWS, 256), F32),
        pltpu.ACC(1)((V_ROWS, 256), F32),
        pltpu.ACC(0)((V_ROWS, 256), F32),
        pltpu.ACC(1)((V_ROWS, 256), F32),
    )


def count_call(start, lists, got, own):
    vmem = pl.BlockSpec(memory_space=pltpu.VMEM)
    return pl.pallas_call(
        count_kernel,
        out_shape=jax.ShapeDtypeStruct((SUBREGIONS, 32, 256), F32),
        in_specs=[pl.BlockSpec(memory_space=pltpu.SMEM), vmem, vmem, vmem],
        out_specs=vmem,
        scratch_shapes=[
            pltpu.VMEM((DUMMY + 1, 8, 128), F32),
            pltpu.VMEM((32, 256), jnp.int32),
            pltpu.SMEM((32, 256), jnp.int32),
            pltpu.VMEM((2, 256, 128 * TILES), BF16),
            pltpu.VMEM((2, V_ROWS, 128 * TILES), BF16),
            pltpu.SemaphoreType.DMA,
        ],
    )(start, lists, got, own)


MESH = pl.DeviceIdType.MESH


def halo_kernel(lists_ref, got_ref, send_sem, recv_sem):
    shell, sky = lax.axis_index("shell"), lax.axis_index("sky")
    shells, skies = lax.axis_size("shell"), lax.axis_size("sky")
    barrier = pltpu.get_barrier_semaphore()

    def present(da, db):
        a, b = shell + da, sky + db
        return (a >= 0) & (a < shells) & (b >= 0) & (b < skies)

    for da, db in DIRS:

        @pl.when(present(da, db))
        def _():
            pl.semaphore_signal(barrier, inc=1, device_id=(shell + da, sky + db), device_id_type=MESH)

    for d, (da, db) in enumerate(DIRS):

        @pl.when(jnp.logical_not(present(da, db)))
        def _():
            got_ref[d] = jnp.zeros((4, PART_DEV), F32)

    beside_shell = 1 + (shell > 0).astype(jnp.int32) + (shell < shells - 1).astype(jnp.int32)
    beside_sky = 1 + (sky > 0).astype(jnp.int32) + (sky < skies - 1).astype(jnp.int32)
    pl.semaphore_wait(barrier, beside_shell * beside_sky - 1)

    def copy(d):
        da, db = DIRS[d]
        return pltpu.make_async_remote_copy(
            src_ref=lists_ref.at[d],
            dst_ref=got_ref.at[7 - d],
            send_sem=send_sem.at[d],
            recv_sem=recv_sem.at[7 - d],
            device_id=(shell + da, sky + db),
            device_id_type=MESH,
        )

    for d, (da, db) in enumerate(DIRS):

        @pl.when(present(da, db))
        def _():
            copy(d).start()

    for d, (da, db) in enumerate(DIRS):

        @pl.when(present(da, db))
        def _():
            copy(d).wait_send()

        @pl.when(present(-da, -db))
        def _():
            copy(d).wait_recv()


def halo_call(lists):
    return pl.pallas_call(
        halo_kernel,
        out_shape=jax.ShapeDtypeStruct((8, 4, PART_DEV), F32),
        in_specs=[pl.BlockSpec(memory_space=pltpu.VMEM)],
        out_specs=pl.BlockSpec(memory_space=pltpu.VMEM),
        scratch_shapes=[pltpu.SemaphoreType.DMA((8,)), pltpu.SemaphoreType.DMA((8,))],
        compiler_params=pltpu.CompilerParams(collective_id=0, has_side_effects=True),
    )(lists)


def total_kernel(skies, counts_ref, own_ref, total_ref, sent_ref, land_ref, send_sem, recv_sem):
    shell, sky = lax.axis_index("shell"), lax.axis_index("sky")
    barrier = pltpu.get_barrier_semaphore()
    for k in range(1, skies):
        pl.semaphore_signal(barrier, inc=1, device_id=(shell, lax.rem(sky + k, skies)), device_id_type=MESH)
    lane_in = lax.broadcasted_iota(jnp.int32, (256, 128), 0)
    lane_out = lax.broadcasted_iota(jnp.int32, (256, 128), 1)
    packed = jnp.zeros((8 * SUBREGIONS, 128), F32)
    for k in range(4):
        rows = jnp.concatenate([counts_ref[r, 8 * k : 8 * k + 8, :] for r in range(SUBREGIONS)], axis=0)
        pick = jnp.where((lane_in >> 3) + 32 * k == lane_out, 1.0, 0.0)
        packed = packed + jnp.dot(rows, pick, precision=lax.Precision.HIGHEST, preferred_element_type=F32)
    own_ref[...] = packed
    mine = packed[0:8]
    for r in range(1, SUBREGIONS):
        mine = mine + packed[8 * r : 8 * r + 8]
    sent_ref[...] = mine
    pl.semaphore_wait(barrier, skies - 1)

    def copy(k):
        return pltpu.make_async_remote_copy(
            src_ref=sent_ref,
            dst_ref=land_ref.at[k - 1],
            send_sem=send_sem.at[k - 1],
            recv_sem=recv_sem.at[k - 1],
            device_id=(shell, lax.rem(sky + k, skies)),
            device_id_type=MESH,
        )

    for k in range(1, skies):
        copy(k).start()
    total = mine
    for k in range(1, skies):
        copy(k).wait_recv()
        total = total + land_ref[k - 1]
    total_ref[...] = total
    for k in range(1, skies):
        copy(k).wait_send()


def total_call(counts):
    skies = lax.axis_size("sky")
    vmem = pl.BlockSpec(memory_space=pltpu.VMEM)
    return pl.pallas_call(
        functools.partial(total_kernel, skies),
        out_shape=(jax.ShapeDtypeStruct((8 * SUBREGIONS, 128), F32), jax.ShapeDtypeStruct((8, 128), F32)),
        in_specs=[vmem],
        out_specs=(vmem, vmem),
        scratch_shapes=[
            pltpu.VMEM((8, 128), F32),
            pltpu.VMEM((skies - 1, 8, 128), F32),
            pltpu.SemaphoreType.DMA((skies - 1,)),
            pltpu.SemaphoreType.DMA((skies - 1,)),
        ],
        compiler_params=pltpu.CompilerParams(collective_id=1, has_side_effects=True),
    )(counts)


def edge_values():
    return [int(4.0 * 10.0 ** (4.0 * level / S_BINS) + 0.5) for level in range(S_BINS + 1)]


def bin_scale(patches):
    edges = edge_values()
    factor = SIDE_CELLS * SIDE_CELLS * SPAN_CELLS / (patches * PART_DEV * PART_DEV)
    values = []
    for level in range(S_BINS):
        volume = 4.0 * math.pi / 3.0 * (edges[level + 1] ** 1.5 - edges[level] ** 1.5) / MU_BINS
        values = values + [factor / volume] * MU_BINS
    return jnp.asarray(values, dtype=F32)


def unpacked(x):
    x = x.reshape(-1, 8, 4, 32).transpose(0, 3, 2, 1).reshape(-1, 32, 32)
    return x[:, :LEVELS_U, :LEVELS_V].reshape(-1, S_BINS * MU_BINS)


def local(coords, weights, live):
    lists, own, start = sort_call(coords.reshape(3, PART_DEV), weights.reshape(1, PART_DEV), live)
    counts = count_call(start, lists, halo_call(lists), own)
    packed, total = total_call(counts)
    leave = total[None] - packed.reshape(SUBREGIONS, 8, 128)
    return (unpacked(leave) * bin_scale(lax.axis_size("sky"))[None, :])[None]


def solution(mesh):
    in_specs = (P(None, "shell", "sky", None), P("shell", "sky", None), P("shell", "sky"))
    out_specs = P("shell", "sky", None)
    return jax.shard_map(local, mesh=mesh, in_specs=in_specs, out_specs=out_specs, check_vma=False)
```

time: 248 us -> 63.7 us (0.26)
  starting transfers between devices: 126 us -> 0 us
  matrix products: 62.5 us -> 0 us
  Pallas kernels: 0 us -> 58.3 us
  other arithmetic: 38.2 us -> 0.62 us
  waiting for transfers between devices: 13.7 us -> 0 us
  local copies, waits for them, and re-layouts: 5.97 us -> 2.99 us
    all_to_all x1 -> x0, starting transfers between devices: 114 us -> none  [from_everyone(): return lax.all_to_all(copies, axis, split_axis=0, concat_axis=0, tiled=True)]
    dot_general x9 -> x0, matrix products: 62.5 us -> none  [pair_block(): jnp.einsum('ijs,ijm->ism', s_weighted, mu_hot, preferred_element_type=jnp...]
    pallas_call x0 -> x4, Pallas kernels: none -> 58.3 us  [the longest x1 26.8 us: total_call(): pl.pallas_call(functools.partial(total_kernel, skies), out_shape=(jax.Sha...]
    add x10 -> x0, other arithmetic: 29.4 us -> none  [the longest x9 29.3 us: pair_block(): s_index = s_index + (squared >= edges[level]).astype(jnp.int32)]
    ppermute x4 -> x0, starting transfers between devices: 12.3 us -> none  [the longest x2 7.73 us: padded(): lax.ppermute(lax.slice_in_dim(block, block.shape[dim] - width, None, axis...]
    all_to_all x1 -> x0, waiting for transfers between devices: 9.64 us -> none  [from_everyone(): return lax.all_to_all(copies, axis, split_axis=0, concat_axis=0, tiled=True)]
    and x9 -> x0, other arithmetic: 5.04 us -> none  [pair_block(): inside = (squared >= edges[0]) & (squared < edges[S_BINS])]
    ppermute x4 -> x0, waiting for transfers between devices: 4.03 us -> none  [the longest x2 4.03 us: padded(): lax.ppermute(lax.slice_in_dim(block, block.shape[dim] - width, None, axis...]
  transfers between devices with their start and end apart: 5 -> 0, of which waited for: 3 -> 0; matrix products, arithmetic and copies ran while one was open for 1% -> 0% of each run, Pallas kernels for 0% -> 0%
where the time goes in v1:
time: 63.7 us; the launch traced here: 62.6 us
  Pallas kernels  58.3 us (92%)
  local copies, waits for them, and re-layouts  2.99 us (5%)
  between operations  0.71 us (1%)
    pallas_call x1, Pallas kernels, total_call(): pl.pallas_call(functools.partial(total_kernel, skies), out_shape=(jax.Sha...  26.8 us
    pallas_call x1, Pallas kernels, count_call(): pl.pallas_call(count_kernel, out_shape=jax.ShapeDtypeStruct((SUBREGIONS,...  15.6 us
    pallas_call x1, Pallas kernels, halo_call(): pl.pallas_call(halo_kernel, out_shape=jax.ShapeDtypeStruct((8, 4, PART_DE...  11.7 us
    pallas_call x1, Pallas kernels, sort_call(): pl.pallas_call(sort_kernel, out_shape=(jax.ShapeDtypeStruct((9, 4, PART_D...  4.22 us
    unnamed x5, local copies, waits for them, and re-layouts  1.89 us

profile of v1, /device:TPU:2, one launch (start us, length us, event | category | flops | bytes accessed | tf_op | source)
XLA Modules:
  0.0 62.6 jit_solution(14189195357747600870)
XLA Ops:
  0.7 1.3 %copy.15 = s32[3,1,1,512]{3,0,1,2:T(4,128)} copy(s32[3,1,1,512]{3,2,1,0:T(1,128)} %param.4) | data formatting | bytes 12288
  1.9 4.2 %shard_map.46 = (f32[9,4,512]{2,1,0:T(4,128)}, f32[4,24,8,128]{3,2,1,0:T(8,128)}, s32[8,128]{1,0:T(8,128)}) custom-call(s32[1,1]{1,0:T(1,128)S(6)} %copy.16.live_ref, s32[3,512]{1,0:T(4,128)} %bitcast.10, bf16[1,512]{1,0:T(2,128)(2,1)} %bitcast.11), custom_call_target="tpu_custom_call" | custom-call | tf_op jit(solution)/shard_map/pallas_call | solution.py:136
  6.2 11.7 %shard_map.47.got_ref = f32[8,4,512]{2,1,0:T(4,128)} custom-call(f32[9,4,512]{2,1,0:T(4,128)} %get-tuple-element.11.lists_ref), custom_call_target="tpu_custom_call" | custom-call | tf_op jit(solution)/shard_map/pallas_call | solution.py:380
  17.9 15.6 %shard_map.48.counts_ref = f32[8,32,256]{2,1,0:T(8,128)} custom-call(s32[8,128]{1,0:T(8,128)} %get-tuple-element.10.start_ref, f32[9,4,512]{2,1,0:T(4,128)} %get-tuple-element.11.lists_ref, f32[8,4,512]{2,1,0:T(4,128)} %shard_map.47.got_ref, f32[4,24,8,128]{3,2,1,0:T(8,128)} %get-tuple-element.12.own_ref), custom_call_target="tpu_custom_call" | custom-call | tf_op jit(solution)/shard_map/pallas_call | solution.py:307
  33.5 26.8 %shard_map.49 = (f32[64,128]{1,0:T(8,128)}, f32[8,128]{1,0:T(8,128)}) custom-call(f32[8,32,256]{2,1,0:T(8,128)} %shard_map.48.counts_ref), custom_call_target="tpu_custom_call" | custom-call | tf_op jit(solution)/shard_map/pallas_call | solution.py:433
  60.3 0.0 copy-start
  60.3 0.8 %sub.11 = f32[8,4,32]{2,1,0:T(4,128)S(1)} reshape(f32[8,128]{1,0:T(8,128)} %get-tuple-element.13) | data formatting | bytes 8192 | tf_op jit(solution)/shard_map/sub | solution.py:471
  61.1 0.0 copy-done
  61.1 0.1 reshape.54
  61.2 0.1 copy.9
  61.3 0.0 copy-start.1
  61.3 0.1 reshape.56
  61.4 0.6 copy-done.1
  62.0 0.6 broadcast_multiply_fusion
  (2 shorter events, 0.0 us)
Async XLA Ops:
  60.3 0.8 %copy-start = (f32[64,128]{1,0:T(8,128)S(1)}, f32[64,128]{1,0:T(8,128)}, u32[]{:S(2)}) copy-start(f32[64,128]{1,0:T(8,128)} %get-tuple-element.14) | copy-start | bytes 98308
  61.3 0.7 %copy-start.1 = (f32[600]{0:T(1024)S(1)}, f32[600]{0:T(1024)}, u32[]{:S(2)}) copy-start(f32[600]{0:T(1024)} %constant.2.clone) | copy-start | bytes 7204

commit v2 on v1

--- a/solution.py
+++ b/solution.py
@@ -25,15 +25,15 @@
         for acc in (acc0, acc1, acc2, acc3, tall0, tall1):
             pltpu.matmul_pop(acc)
         n = PART_DEV
-        x = (coords_ref[0:1, :] & (SIDE_CELLS - 1)).astype(F32)
-        y = (coords_ref[1:2, :] & (SIDE_CELLS - 1)).astype(F32)
-        zi = coords_ref[2:3, :]
+        x = (coords_ref[0, 0] & (SIDE_CELLS - 1)).astype(F32)
+        y = (coords_ref[1, 0] & (SIDE_CELLS - 1)).astype(F32)
+        zi = coords_ref[2, 0]
         region = zi >> 7
         z_high = region.astype(F32)
         z_low = (zi & 127).astype(F32)
         slot = lax.broadcasted_iota(jnp.int32, (1, n), 1)
         alive = slot < live_ref[0, 0]
-        w = jnp.where(alive, weight_ref[0:1, :].astype(F32), 0.0)
+        w = jnp.where(alive, weight_ref[0].astype(F32), 0.0)
         key = (jnp.where(alive, zi * n, SPAN_CELLS * n) + slot).astype(F32)
         key_column = jnp.transpose(jnp.broadcast_to(key, (128, n)))[:, 0:1]
         before = jnp.where(key_column < key, 1.0, 0.0).astype(BF16)
@@ -146,6 +146,7 @@
             pl.BlockSpec(memory_space=pltpu.VMEM),
         ],
         out_specs=[pl.BlockSpec(memory_space=pltpu.VMEM)] * 3,
+        compiler_params=pltpu.CompilerParams(vmem_limit_bytes=8 << 20),
     )(live, coords, weights)
 
 
@@ -158,8 +159,8 @@
 DUMMY = 9 * ROWS
 
 
-def count_kernel(start_ref, lists_ref, got_ref, own_ref, out_ref, rows_ref, table_ref, table_sm, hot_u, hot_v, sem):
-    def body(a0, a1, b0, b1):
+def count_kernel(start_ref, lists_ref, got_ref, own_ref, out_ref, rows_ref, table_ref, table_sm, sem):
+    def body(a0, a1, b0, b1, hot_u, hot_v, bin_u, bin_v, far_w, own_w):
         sets = ((a0, a1), (b0, b1))
         for acc in (a0, a1, b0, b1):
             pltpu.matmul_pop(acc)
@@ -222,50 +223,59 @@
 
         stop = start_ref[0, SUBREGIONS]
 
-        def fill(state, buf):
+        def index(state):
             g, b = state
-            group = jnp.minimum(g, GROUPS - 1)
-            xi, yi, zi, wi = own_ref[0, group], own_ref[1, group], own_ref[2, group], own_ref[3, group]
-            w_own = jnp.concatenate([wi, wi], axis=0).astype(BF16)
+            for half in range(2):
+                group = jnp.minimum(g, GROUPS - 1)
+                xi, yi, zi, wi = own_ref[0, group], own_ref[1, group], own_ref[2, group], own_ref[3, group]
+                own_w[half] = jnp.concatenate([wi, wi], axis=0).astype(BF16)
+                for t in range(TILES):
+                    row = table_sm[g, TILES * b + t]
+                    dx = xi - rows_ref[row, 0:1, :]
+                    dy = yi - rows_ref[row, 1:2, :]
+                    dz = zi - rows_ref[row, 2:3, :]
+                    far_w[half, t] = jnp.broadcast_to(rows_ref[row, 3:4, :].astype(BF16), (16, 128))
+                    dx2 = dx * dx
+                    q = dx2 + dy * dy + dz * dz
+                    s = jnp.floor(jnp.log2(q + 0.48) * LOG_SCALE + LOG_BASE)
+                    near = jnp.floor(jnp.abs(dx) * lax.rsqrt(q) * float(MU_BINS) + 0.5)
+                    mu = jnp.where(near * near * q > dx2 * float(MU_BINS * MU_BINS), near - 1.0, near)
+                    c = s * float(MU_BINS) + jnp.minimum(mu, MU_BINS - 1.0)
+                    u = jnp.floor(c * (1.0 / LEVELS_V) + 0.01)
+                    v = c - u * float(LEVELS_V)
+                    bin_u[half, t] = jnp.concatenate([u, u - 1.0], axis=0).astype(BF16)
+                    bin_v[half, t] = jnp.concatenate([v, v - 1.0], axis=0).astype(BF16)
+                b = b + 1
+                over = b >= table_sm[g, 255]
+                g = jnp.where(over, g + 1, g)
+                g = jnp.where(g >= stop, GROUPS, g)
+                b = jnp.where(over, 0, b)
+            return g, b
+
+        def fill(half):
+            w_own = own_w[half]
             for t in range(TILES):
-                row = table_sm[g, TILES * b + t]
-                dx = xi - rows_ref[row, 0:1, :]
-                dy = yi - rows_ref[row, 1:2, :]
-                dz = zi - rows_ref[row, 2:3, :]
-                w_far = jnp.broadcast_to(rows_ref[row, 3:4, :].astype(BF16), (16, 128))
-                dx2 = dx * dx
-                q = dx2 + dy * dy + dz * dz
-                s = jnp.floor(jnp.log2(q + 0.48) * LOG_SCALE + LOG_BASE)
-                near = jnp.floor(jnp.abs(dx) * lax.rsqrt(q) * float(MU_BINS) + 0.5)
-                mu = jnp.where(near * near * q > dx2 * float(MU_BINS * MU_BINS), near - 1.0, near)
-                c = s * float(MU_BINS) + jnp.minimum(mu, MU_BINS - 1.0)
-                u = jnp.floor(c * (1.0 / LEVELS_V) + 0.01)
-                v = c - u * float(LEVELS_V)
-                u2 = jnp.concatenate([u, u - 1.0], axis=0).astype(BF16)
-                v2 = jnp.concatenate([v, v - 1.0], axis=0).astype(BF16)
+                u2, v2, w_far = bin_u[half, t], bin_v[half, t], far_w[half, t]
                 lanes = slice(128 * t, 128 * t + 128)
                 for k in range(LEVELS_U // 2):
-                    hot_u[buf, 16 * k : 16 * k + 16, lanes] = jnp.where(u2 == jnp.bfloat16(2 * k), w_far, zero)
+                    hot_u[half, 16 * k : 16 * k + 16, lanes] = jnp.where(u2 == jnp.bfloat16(2 * k), w_far, zero)
                 for k in range(V_ROWS // 16):
-                    hot_v[buf, 16 * k : 16 * k + 16, lanes] = jnp.where(v2 == jnp.bfloat16(2 * k), w_own, zero)
-            b = b + 1
-            over = b >= table_sm[g, 255]
-            g = jnp.where(over, g + 1, g)
-            g = jnp.where(g >= stop, GROUPS, g)
-            return g, jnp.where(over, 0, b)
-
-        def push(buf):
+                    hot_v[half, 16 * k : 16 * k + 16, lanes] = jnp.where(v2 == jnp.bfloat16(2 * k), w_own, zero)
+
+        def push(half):
             for mxu in range(2):
-                pltpu.matmul_push_rhs(hot_u[buf, :, 256 * mxu : 256 * mxu + 256], staging_register=buf, mxu_index=mxu, transpose=True)
-
-        def multiply(buf, accs):
+                pltpu.matmul_push_rhs(hot_u[half, :, 256 * mxu : 256 * mxu + 256], staging_register=half, mxu_index=mxu, transpose=True)
+
+        def multiply(half, accs):
             for mxu in range(2):
-                pltpu.matmul_acc_lhs(accs[mxu], hot_v[buf, :, 256 * mxu : 256 * mxu + 256], load_staged_rhs=buf)
+                pltpu.matmul_acc_lhs(accs[mxu], hot_v[half, :, 256 * mxu : 256 * mxu + 256], load_staged_rhs=half)
 
         state = (jnp.where(stop > 0, 0, GROUPS).astype(jnp.int32), jnp.int32(0))
-        state = fill(state, 0)
-        push(0)
-        state = fill(state, 1)
+        state = index(state)
+        for half in range(2):
+            fill(half)
+            push(half)
+        state = index(state)
         sub = lax.broadcasted_iota(jnp.int32, (8, 256), 0)
         diagonal = sub == (lax.broadcasted_iota(jnp.int32, (8, 256), 1) & 7)
 
@@ -280,17 +290,18 @@
             accs = sets[r % 2]
 
             def trip(_, state):
-                push(1)
-                multiply(0, accs)
-                state = fill(state, 0)
-                push(0)
-                multiply(1, accs)
-                return fill(state, 1)
+                for half in range(2):
+                    multiply(half, accs)
+                for half in range(2):
+                    fill(half)
+                    push(half)
+                return index(state)
 
             state = lax.fori_loop(0, trips[r], trip, state)
             if r > 0:
                 drain(r - 1)
-        multiply(0, sets[(SUBREGIONS - 1) % 2])
+        for half in range(2):
+            multiply(half, sets[(SUBREGIONS - 1) % 2])
         drain(SUBREGIONS - 1)
 
     pl.run_scoped(
@@ -299,6 +310,12 @@
         pltpu.ACC(1)((V_ROWS, 256), F32),
         pltpu.ACC(0)((V_ROWS, 256), F32),
         pltpu.ACC(1)((V_ROWS, 256), F32),
+        pltpu.VMEM((2, 256, 128 * TILES), BF16),
+        pltpu.VMEM((2, V_ROWS, 128 * TILES), BF16),
+        pltpu.VMEM((2, TILES, 16, 128), BF16),
+        pltpu.VMEM((2, TILES, 16, 128), BF16),
+        pltpu.VMEM((2, TILES, 16, 128), BF16),
+        pltpu.VMEM((2, 16, 128), BF16),
     )
 
 
@@ -313,10 +330,9 @@
             pltpu.VMEM((DUMMY + 1, 8, 128), F32),
             pltpu.VMEM((32, 256), jnp.int32),
             pltpu.SMEM((32, 256), jnp.int32),
-            pltpu.VMEM((2, 256, 128 * TILES), BF16),
-            pltpu.VMEM((2, V_ROWS, 128 * TILES), BF16),
             pltpu.SemaphoreType.DMA,
         ],
+        compiler_params=pltpu.CompilerParams(vmem_limit_bytes=8 << 20),
     )(start, lists, got, own)
 
 
@@ -383,7 +399,7 @@
         in_specs=[pl.BlockSpec(memory_space=pltpu.VMEM)],
         out_specs=pl.BlockSpec(memory_space=pltpu.VMEM),
         scratch_shapes=[pltpu.SemaphoreType.DMA((8,)), pltpu.SemaphoreType.DMA((8,))],
-        compiler_params=pltpu.CompilerParams(collective_id=0, has_side_effects=True),
+        compiler_params=pltpu.CompilerParams(collective_id=0, has_side_effects=True, vmem_limit_bytes=4 << 20),
     )(lists)
 
 
@@ -441,7 +457,7 @@
             pltpu.SemaphoreType.DMA((skies - 1,)),
             pltpu.SemaphoreType.DMA((skies - 1,)),
         ],
-        compiler_params=pltpu.CompilerParams(collective_id=1, has_side_effects=True),
+        compiler_params=pltpu.CompilerParams(collective_id=1, has_side_effects=True, vmem_limit_bytes=4 << 20),
     )(counts)
 
 
@@ -465,7 +481,7 @@
 
 
 def local(coords, weights, live):
-    lists, own, start = sort_call(coords.reshape(3, PART_DEV), weights.reshape(1, PART_DEV), live)
+    lists, own, start = sort_call(coords, weights, live)
     counts = count_call(start, lists, halo_call(lists), own)
     packed, total = total_call(counts)
     leave = total[None] - packed.reshape(SUBREGIONS, 8, 128)

time: 63.7 us -> 48 us (0.75); the launches traced: 62.6 us -> 48 us
  Pallas kernels: 58.3 us -> 44.3 us
    pallas_call x1, Pallas kernels: 26.8 us -> 14.7 us  [total_call(): pl.pallas_call(functools.partial(total_kernel, skies), out_shape=(jax.Sha...]
    pallas_call x1, Pallas kernels: 4.22 us -> 2.74 us  [sort_call(): pl.pallas_call(sort_kernel, out_shape=(jax.ShapeDtypeStruct((9, 4, PART_D...]
    pallas_call x1, Pallas kernels: 11.7 us -> 10.3 us  [halo_call(): pl.pallas_call(halo_kernel, out_shape=jax.ShapeDtypeStruct((8, 4, PART_DE...]
    pallas_call x1, Pallas kernels: 15.6 us -> 16.6 us  [count_call(): pl.pallas_call(count_kernel, out_shape=jax.ShapeDtypeStruct((SUBREGIONS,...]
    sub x2, local copies, waits for them, and re-layouts: 0.77 us -> 0.08 us  [local(): leave = total[None] - packed.reshape(SUBREGIONS, 8, 128)]
    unnamed x5 -> x6, local copies, waits for them, and re-layouts: 1.89 us -> 1.96 us
where the time goes in v2:
time: 48 us
  Pallas kernels  44.3 us (92%)
  local copies, waits for them, and re-layouts  2.37 us (5%)
  between operations  0.72 us (2%)
  other arithmetic  0.62 us (1%)
    pallas_call x1, Pallas kernels, count_call(): pl.pallas_call(count_kernel, out_shape=jax.ShapeDtypeStruct((SUBREGIONS,...  16.6 us
    pallas_call x1, Pallas kernels, total_call(): pl.pallas_call(functools.partial(total_kernel, skies), out_shape=(jax.Sha...  14.7 us
    pallas_call x1, Pallas kernels, halo_call(): pl.pallas_call(halo_kernel, out_shape=jax.ShapeDtypeStruct((8, 4, PART_DE...  10.3 us
    pallas_call x1, Pallas kernels, sort_call(): pl.pallas_call(sort_kernel, out_shape=(jax.ShapeDtypeStruct((9, 4, PART_D...  2.74 us
    unnamed x6, local copies, waits for them, and re-layouts  1.96 us

profile of v2, /device:TPU:2, one launch (start us, length us, event | category | flops | bytes accessed | tf_op | source)
XLA Modules:
  0.0 48.0 jit_solution(13320736499604412342)
XLA Ops:
  0.7 0.0 copy-start
  0.7 0.7 %copy-done = s32[3,1,1,512]{3,2,1,0:T(1,128)S(1)} copy-done((s32[3,1,1,512]{3,2,1,0:T(1,128)S(1)}, s32[3,1,1,512]{3,2,1,0:T(1,128)}, u32[]{:S(2)}) %copy-start) | copy-done | bytes 6168
  1.3 0.0 copy-start.1
  1.3 0.7 %copy-done.1 = bf16[1,1,512]{2,1,0:T(2,128)(2,1)S(1)} copy-done((bf16[1,1,512]{2,1,0:T(2,128)(2,1)S(1)}, bf16[1,1,512]{2,1,0:T(2,128)(2,1)}, u32[]{:S(2)}) %copy-start.1) | copy-done | bytes 1048
  2.0 2.7 %shard_map.46 = (f32[9,4,512]{2,1,0:T(4,128)S(1)}, f32[4,24,8,128]{3,2,1,0:T(8,128)S(1)}, s32[8,128]{1,0:T(8,128)S(1)}) custom-call(s32[1,1]{1,0:T(1,128)S(6)} %copy.13.live_ref, s32[3,1,1,512]{3,2,1,0:T(1,128)S(1)} %copy-done, bf16[1,1,512]{2,1,0:T(2,128)(2,1)S(1)} %copy-done.1), custom_call_target="tpu_custom_call" | custom-call | tf_op jit(solution)/shard_map/pallas_call | solution.py:136
  4.8 10.3 %shard_map.47.got_ref = f32[8,4,512]{2,1,0:T(4,128)S(1)} custom-call(f32[9,4,512]{2,1,0:T(4,128)S(1)} %get-tuple-element.11.lists_ref), custom_call_target="tpu_custom_call" | custom-call | tf_op jit(solution)/shard_map/pallas_call | solution.py:396
  15.1 16.6 %shard_map.48.counts_ref = f32[8,32,256]{2,1,0:T(8,128)S(1)} custom-call(s32[8,128]{1,0:T(8,128)S(1)} %get-tuple-element.10.start_ref, f32[9,4,512]{2,1,0:T(4,128)S(1)} %get-tuple-element.11.lists_ref, f32[8,4,512]{2,1,0:T(4,128)S(1)} %shard_map.47.got_ref, f32[4,24,8,128]{3,2,1,0:T(8,128)S(1)} %get-tuple-element.12.own_ref), custom_call_target="tpu_custom_call" | custom-call | tf_op jit(solution)/shard_map/pallas_call | solution.py:324
  31.7 14.7 %shard_map.49 = (f32[64,128]{1,0:T(8,128)S(1)}, f32[8,128]{1,0:T(8,128)S(1)}) custom-call(f32[8,32,256]{2,1,0:T(8,128)S(1)} %shard_map.48.counts_ref), custom_call_target="tpu_custom_call" | custom-call | tf_op jit(solution)/shard_map/pallas_call | solution.py:449
  46.3 0.1 sub.11
  46.4 0.1 reshape.46
  46.6 0.1 copy.9
  46.7 0.0 copy-start.2
  46.7 0.1 reshape.48
  46.8 0.6 %copy-done.2 = f32[600]{0:T(1024)S(1)} copy-done((f32[600]{0:T(1024)S(1)}, f32[600]{0:T(1024)}, u32[]{:S(2)}) %copy-start.2) | copy-done | bytes 2424
  47.4 0.6 %broadcast_multiply_fusion = f32[1,8,600]{2,1,0:T(8,128)} fusion(f32[1,8,600]{2,1,0:T(8,128)S(1)} %reshape.48, f32[600]{0:T(1024)S(1)} %copy-done.2), kind=kLoop, calls=%fused_computation.2 | loop fusion | flops 4800 | bytes 40800 | tf_op jit(solution)/shard_map/mul | solution.py:488
  (2 shorter events, 0.0 us)
Async XLA Ops:
  0.7 0.7 %copy-start = (s32[3,1,1,512]{3,2,1,0:T(1,128)S(1)}, s32[3,1,1,512]{3,2,1,0:T(1,128)}, u32[]{:S(2)}) copy-start(s32[3,1,1,512]{3,2,1,0:T(1,128)} %coords_ref.1) | copy-start | bytes 18436
  1.3 0.7 %copy-start.1 = (bf16[1,1,512]{2,1,0:T(2,128)(2,1)S(1)}, bf16[1,1,512]{2,1,0:T(2,128)(2,1)}, u32[]{:S(2)}) copy-start(bf16[1,1,512]{2,1,0:T(2,128)(2,1)} %weight_ref.1) | copy-start | bytes 3076
  46.7 0.7 %copy-start.2 = (f32[600]{0:T(1024)S(1)}, f32[600]{0:T(1024)}, u32[]{:S(2)}) copy-start(f32[600]{0:T(1024)} %constant.2.clone) | copy-start | bytes 7204

commit v3 on v2

--- a/solution.py
+++ b/solution.py
@@ -15,15 +15,57 @@
 GROUPS = 24
 STEP = 16
 ROWS = PART_DEV // STEP
+DUMMY = 9 * ROWS
+TILES = 4
 DIRS = tuple((da, db) for da in (-1, 0, 1) for db in (-1, 0, 1) if (da, db) != (0, 0))
+MESH = pl.DeviceIdType.MESH
 F32 = jnp.float32
 BF16 = jnp.bfloat16
 
 
-def sort_kernel(live_ref, coords_ref, weight_ref, lists_ref, own_ref, start_ref):
+def send_kernel(coords_hbm, weight_hbm, live_hbm, table_ref, rows_ref, own_ref, coords_ref, weight_ref, live_ref, lists_ref, got_ref, load_sem, send_sem, recv_sem):
+    shell, sky = lax.axis_index("shell"), lax.axis_index("sky")
+    shells, skies = lax.axis_size("shell"), lax.axis_size("sky")
+    barrier = pltpu.get_barrier_semaphore()
+    loads = [
+        pltpu.make_async_copy(src, dst, load_sem.at[k])
+        for k, (src, dst) in enumerate(((coords_hbm, coords_ref), (weight_hbm, weight_ref), (live_hbm, live_ref)))
+    ]
+    for load in loads:
+        load.start()
+
+    def present(da, db):
+        a, b = shell + da, sky + db
+        return (a >= 0) & (a < shells) & (b >= 0) & (b < skies)
+
+    for da, db in DIRS:
+
+        @pl.when(present(da, db))
+        def _():
+            pl.semaphore_signal(barrier, inc=1, device_id=(shell + da, sky + db), device_id_type=MESH)
+
+    for d, (da, db) in enumerate(DIRS):
+
+        @pl.when(jnp.logical_not(present(da, db)))
+        def _():
+            got_ref[d] = jnp.zeros((4, PART_DEV), F32)
+
+    def copy(d):
+        da, db = DIRS[d]
+        return pltpu.make_async_remote_copy(
+            src_ref=lists_ref.at[d],
+            dst_ref=got_ref.at[7 - d],
+            send_sem=send_sem.at[d],
+            recv_sem=recv_sem.at[7 - d],
+            device_id=(shell + da, sky + db),
+            device_id_type=MESH,
+        )
+
     def body(acc0, acc1, acc2, acc3, tall0, tall1):
         for acc in (acc0, acc1, acc2, acc3, tall0, tall1):
             pltpu.matmul_pop(acc)
+        for load in loads:
+            load.wait()
         n = PART_DEV
         x = (coords_ref[0, 0] & (SIDE_CELLS - 1)).astype(F32)
         y = (coords_ref[1, 0] & (SIDE_CELLS - 1)).astype(F32)
@@ -32,7 +74,7 @@
         z_high = region.astype(F32)
         z_low = (zi & 127).astype(F32)
         slot = lax.broadcasted_iota(jnp.int32, (1, n), 1)
-        alive = slot < live_ref[0, 0]
+        alive = slot < live_ref[...]
         w = jnp.where(alive, weight_ref[0].astype(F32), 0.0)
         key = (jnp.where(alive, zi * n, SPAN_CELLS * n) + slot).astype(F32)
         key_column = jnp.transpose(jnp.broadcast_to(key, (128, n)))[:, 0:1]
@@ -79,6 +121,16 @@
                 lists_ref[d, 1:2, lanes] = got[1:2] - float(SIDE_CELLS * db)
                 lists_ref[d, 2:3, lanes] = got[2:3] * 128.0 + got[3:4]
                 lists_ref[d, 3:4, lanes] = got[4:5]
+
+        beside_shell = 1 + (shell > 0).astype(jnp.int32) + (shell < shells - 1).astype(jnp.int32)
+        beside_sky = 1 + (sky > 0).astype(jnp.int32) + (sky < skies - 1).astype(jnp.int32)
+        pl.semaphore_wait(barrier, beside_shell * beside_sky - 1)
+        for d, (da, db) in enumerate(DIRS):
+
+            @pl.when(present(da, db))
+            def _():
+                copy(d).start()
+
         shift = jnp.zeros((1, n), F32)
         first = jnp.zeros((1, 1), F32)
         group = jnp.zeros((1, 1), F32)
@@ -91,11 +143,11 @@
             first = first + count
             group = group + jnp.floor((count + 31.0) * (1.0 / 32.0))
         starts = starts + [group]
-        row = lax.broadcasted_iota(jnp.int32, (8, 128), 1)
-        table = jnp.zeros((8, 128), F32)
-        for r in range(9):
-            table = jnp.where(row == r, starts[r], table)
-        start_ref[...] = table.astype(jnp.int32)
+        lane_row = lax.broadcasted_iota(jnp.int32, (1, 128), 1)
+        begin, end = jnp.zeros((1, 128), F32), jnp.zeros((1, 128), F32)
+        for r in range(SUBREGIONS):
+            begin = jnp.where(lane_row == r, starts[r], begin)
+            end = jnp.where(lane_row == r, starts[r + 1], end)
         target = jnp.where(alive, rank[8:9, :] + shift, -1.0)
         wide = lax.broadcasted_iota(jnp.int32, (GROUPS * 32, 1), 0).astype(F32)
         hot = jnp.where(wide == target, 1.0, 0.0).astype(BF16)
@@ -106,7 +158,7 @@
             for mxu, acc in ((0, tall0), (1, tall1)):
                 pltpu.matmul_push_rhs(rhs[:, cols], staging_register=0, mxu_index=mxu, transpose=True)
                 pltpu.matmul_acc_lhs(acc, hot[half_rows * mxu : half_rows * mxu + half_rows, cols], load_staged_rhs=0)
-        lane = lax.broadcasted_iota(jnp.int32, (8, 128), 1) // 32
+        quarter = lax.broadcasted_iota(jnp.int32, (8, 128), 1) // 32
         for mxu, acc in ((0, tall0), (1, tall1)):
             got = pltpu.matmul_pop(acc)[:, 0:128]
             for g in range(GROUPS // 2):
@@ -118,8 +170,66 @@
                 for k in range(4):
                     value = parts[0][k]
                     for q in range(1, 4):
-                        value = jnp.where(lane == q, parts[q][k], value)
+                        value = jnp.where(quarter == q, parts[q][k], value)
                     own_ref[k, mxu * (GROUPS // 2) + g] = value
+
+        zs, ws = own_ref[2], own_ref[3]
+        z_min = jnp.min(jnp.min(jnp.where(ws > 0.0, zs, 1e6), axis=1), axis=1, keepdims=True)
+        z_max = jnp.max(jnp.max(jnp.where(ws > 0.0, zs, -1e6), axis=1), axis=1, keepdims=True)
+        lane = lax.broadcasted_iota(jnp.int32, (GROUPS, 128), 1)
+        chunk = lane.astype(F32) * 2.0
+        even = jnp.full((GROUPS, 128), float(DUMMY), F32)
+        odd = even
+        total = jnp.zeros((GROUPS, 1), F32)
+        lane8 = lax.broadcasted_iota(jnp.int32, (8, 128), 1)
+        rows_ref[DUMMY] = jnp.zeros((8, 128), F32)
+        for d in (8, 3, 4, 1, 6, 0, 2, 5, 7):
+            if d < 8:
+
+                @pl.when(present(*DIRS[d]))
+                def _():
+                    copy(7 - d).wait_recv()
+
+            src = lists_ref.at[8] if d == 8 else got_ref.at[d]
+            z_row = jnp.where(src[3:4, :] > 0.0, src[2:3, :], 2e6)
+            low = jnp.sum(jnp.where(z_row < z_min - float(REACH), 1.0, 0.0), axis=1, keepdims=True)
+            high = jnp.sum(jnp.where(z_row <= z_max + float(REACH), 1.0, 0.0), axis=1, keepdims=True)
+            first = jnp.floor(low * (1.0 / STEP))
+            count = jnp.where(high > low, jnp.floor((high - STEP * first + 31.0) * (1.0 / 32.0)), 0.0)
+            at = chunk - total
+            even = jnp.where((at >= 0.0) & (at < count), at * 2.0 + (first + float(ROWS * d)), even)
+            at = at + 1.0
+            odd = jnp.where((at >= 0.0) & (at < count), at * 2.0 + (first + float(ROWS * d)), odd)
+            total = total + count
+            parts = []
+            for t in range(4):
+                block = src[:, 128 * t : 128 * t + 128]
+                block = jnp.concatenate([block, block], axis=0)
+                for k in range(4):
+                    part = block if k == 0 else pltpu.roll(block, 128 - 32 * k, 1)
+                    part = jnp.where(lane8 < 32, part, pltpu.roll(part, 32, 1))
+                    part = jnp.where(lane8 < 64, part, pltpu.roll(part, 64, 1))
+                    parts.append(part)
+            turned = [pltpu.roll(part, 16, 1) for part in parts] + [jnp.zeros((8, 128), F32)]
+            for k in range(16):
+                rows_ref[ROWS * d + 2 * k] = parts[k]
+                rows_ref[ROWS * d + 2 * k + 1] = jnp.where((lane8 & 31) < 16, turned[k], turned[k + 1])
+        batches = jnp.floor((total + (TILES - 1.0)) * (1.0 / TILES))
+        name = lax.broadcasted_iota(jnp.int32, (GROUPS, 128), 0).astype(F32)
+        number = jnp.sum(jnp.where((name >= begin) & (name < end), batches, 0.0), axis=0, keepdims=True)
+        extra = number - 2.0 * jnp.floor(number * 0.5)
+        batches = batches + jnp.sum(jnp.where(name == end - 1.0, extra, 0.0), axis=1, keepdims=True)
+        table = jnp.where(lane == 127, batches, even + 512.0 * odd)
+        table_ref[0:GROUPS, :] = table.astype(jnp.int32)
+        idle = jnp.where(lane_row == 127, float(1 << 20), float(DUMMY * 513))
+        trips = jnp.where(lane_row == SUBREGIONS, starts[SUBREGIONS], (number + extra) * 0.5)
+        tail = jnp.concatenate([idle, trips, jnp.zeros((6, 128), F32)], axis=0)
+        table_ref[GROUPS : GROUPS + 8, :] = tail.astype(jnp.int32)
+        for d, (da, db) in enumerate(DIRS):
+
+            @pl.when(present(da, db))
+            def _():
+                copy(d).wait_send()
 
     pl.run_scoped(
         body,
@@ -132,96 +242,51 @@
     )
 
 
-def sort_call(coords, weights, live):
+def send_call(coords, weights, live):
+    far = pl.BlockSpec(memory_space=pltpu.HBM)
     return pl.pallas_call(
-        sort_kernel,
+        send_kernel,
         out_shape=(
-            jax.ShapeDtypeStruct((9, 4, PART_DEV), F32),
+            jax.ShapeDtypeStruct((GROUPS + 8, 128), jnp.int32),
+            jax.ShapeDtypeStruct((DUMMY + 1, 8, 128), F32),
             jax.ShapeDtypeStruct((4, GROUPS, 8, 128), F32),
-            jax.ShapeDtypeStruct((8, 128), jnp.int32),
         ),
-        in_specs=[
-            pl.BlockSpec(memory_space=pltpu.SMEM),
-            pl.BlockSpec(memory_space=pltpu.VMEM),
-            pl.BlockSpec(memory_space=pltpu.VMEM),
+        in_specs=[far] * 3,
+        out_specs=[pl.BlockSpec(memory_space=pltpu.VMEM)] * 3,
+        scratch_shapes=[
+            pltpu.VMEM((3, 1, 1, PART_DEV), jnp.int32),
+            pltpu.VMEM((1, 1, PART_DEV), BF16),
+            pltpu.VMEM((1, 1), jnp.int32),
+            pltpu.VMEM((9, 4, PART_DEV), F32),
+            pltpu.VMEM((8, 4, PART_DEV), F32),
+            pltpu.SemaphoreType.DMA((3,)),
+            pltpu.SemaphoreType.DMA((8,)),
+            pltpu.SemaphoreType.DMA((8,)),
         ],
-        out_specs=[pl.BlockSpec(memory_space=pltpu.VMEM)] * 3,
-        compiler_params=pltpu.CompilerParams(vmem_limit_bytes=8 << 20),
-    )(live, coords, weights)
+        compiler_params=pltpu.CompilerParams(collective_id=0, has_side_effects=True, vmem_limit_bytes=12 << 20),
+    )(coords, weights, live)
 
 
 LOG_SCALE = (S_BINS / 4.0) / math.log2(10.0)
 LOG_BASE = -4.515457845
 LEVELS_U = 24
 LEVELS_V = 25
-TILES = 4
 V_ROWS = 208
-DUMMY = 9 * ROWS
-
-
-def count_kernel(start_ref, lists_ref, got_ref, own_ref, out_ref, rows_ref, table_ref, table_sm, sem):
+
+
+def count_kernel(table_ref, rows_ref, own_ref, out_ref, table_sm, sem):
     def body(a0, a1, b0, b1, hot_u, hot_v, bin_u, bin_v, far_w, own_w):
         sets = ((a0, a1), (b0, b1))
+        copy = pltpu.make_async_copy(table_ref, table_sm, sem)
+        copy.start()
         for acc in (a0, a1, b0, b1):
             pltpu.matmul_pop(acc)
-        zs, ws = own_ref[2], own_ref[3]
-        z_min = jnp.min(jnp.min(jnp.where(ws > 0.0, zs, 1e6), axis=1), axis=1, keepdims=True)
-        z_max = jnp.max(jnp.max(jnp.where(ws > 0.0, zs, -1e6), axis=1), axis=1, keepdims=True)
-        lane = lax.broadcasted_iota(jnp.int32, (GROUPS, 256), 1).astype(F32)
-        table = jnp.full((GROUPS, 256), float(DUMMY), F32)
-        total = jnp.zeros((GROUPS, 1), F32)
-        for d in range(9):
-            src = lists_ref.at[8] if d == 8 else got_ref.at[d]
-            z_row = jnp.where(src[3:4, :] > 0.0, src[2:3, :], 2e6)
-            low = jnp.sum(jnp.where(z_row < z_min - float(REACH), 1.0, 0.0), axis=1, keepdims=True)
-            high = jnp.sum(jnp.where(z_row <= z_max + float(REACH), 1.0, 0.0), axis=1, keepdims=True)
-            first = jnp.floor(low * (1.0 / STEP))
-            count = jnp.where(high > low, jnp.floor((high - STEP * first + 31.0) * (1.0 / 32.0)), 0.0)
-            at = lane - total
-            table = jnp.where((at >= 0.0) & (at < count), at * 2.0 + (first + float(ROWS * d)), table)
-            total = total + count
-        batches = jnp.floor((total + (TILES - 1.0)) * (1.0 / TILES))
-        table = jnp.where(lane == 255.0, batches, table)
-        table_ref[0:GROUPS, :] = table.astype(jnp.int32)
-        tail = lax.broadcasted_iota(jnp.int32, (8, 256), 1)
-        table_ref[GROUPS : GROUPS + 8, :] = jnp.where(tail == 255, 1 << 20, DUMMY)
-        copy = pltpu.make_async_copy(table_ref, table_sm, sem)
-        copy.start()
-        lane = lax.broadcasted_iota(jnp.int32, (8, 128), 1)
-        for d in range(9):
-            src = lists_ref.at[8] if d == 8 else got_ref.at[d]
-            wide = []
-            for t in range(4):
-                block = src[:, 128 * t : 128 * t + 128]
-                block = jnp.concatenate([block, block], axis=0)
-                for k in range(4):
-                    part = block if k == 0 else pltpu.roll(block, 128 - 32 * k, 1)
-                    part = jnp.where(lane < 32, part, pltpu.roll(part, 32, 1))
-                    part = jnp.where(lane < 64, part, pltpu.roll(part, 64, 1))
-                    wide.append(part)
-            turned = [pltpu.roll(part, 16, 1) for part in wide] + [jnp.zeros((8, 128), F32)]
-            for k in range(16):
-                rows_ref[ROWS * d + 2 * k] = wide[k]
-                rows_ref[ROWS * d + 2 * k + 1] = jnp.where((lane & 31) < 16, turned[k], turned[k + 1])
-        rows_ref[DUMMY] = jnp.zeros((8, 128), F32)
-        for buf in range(2):
-            hot_u[buf, 8 * LEVELS_U :, :] = jnp.zeros((256 - 8 * LEVELS_U, 128 * TILES), BF16)
+        for half in range(2):
+            hot_u[half, 8 * LEVELS_U :, :] = jnp.zeros((256 - 8 * LEVELS_U, 128 * TILES), BF16)
         copy.wait()
-        trips = []
-        for r in range(SUBREGIONS):
-            begin, end = start_ref[0, r], start_ref[0, r + 1]
-            number = lax.fori_loop(begin, end, lambda g, n: n + table_sm[g, 255], jnp.int32(0))
-            last = jnp.maximum(end - 1, 0)
-
-            @pl.when(number % 2 == 1)
-            def _():
-                table_sm[last, 255] = table_sm[last, 255] + 1
-
-            trips.append((number + 1) // 2)
-
+        trips = [table_sm[GROUPS + 1, r] for r in range(SUBREGIONS)]
+        stop = table_sm[GROUPS + 1, SUBREGIONS]
         zero = jnp.zeros((16, 128), BF16)
-
-        stop = start_ref[0, SUBREGIONS]
 
         def index(state):
             g, b = state
@@ -230,7 +295,8 @@
                 xi, yi, zi, wi = own_ref[0, group], own_ref[1, group], own_ref[2, group], own_ref[3, group]
                 own_w[half] = jnp.concatenate([wi, wi], axis=0).astype(BF16)
                 for t in range(TILES):
-                    row = table_sm[g, TILES * b + t]
+                    pair = table_sm[g, TILES // 2 * b + t // 2]
+                    row = pair & 511 if t % 2 == 0 else pair >> 9
                     dx = xi - rows_ref[row, 0:1, :]
                     dy = yi - rows_ref[row, 1:2, :]
                     dz = zi - rows_ref[row, 2:3, :]
@@ -246,7 +312,7 @@
                     bin_u[half, t] = jnp.concatenate([u, u - 1.0], axis=0).astype(BF16)
                     bin_v[half, t] = jnp.concatenate([v, v - 1.0], axis=0).astype(BF16)
                 b = b + 1
-                over = b >= table_sm[g, 255]
+                over = b >= table_sm[g, 127]
                 g = jnp.where(over, g + 1, g)
                 g = jnp.where(g >= stop, GROUPS, g)
                 b = jnp.where(over, 0, b)
@@ -319,88 +385,16 @@
     )
 
 
-def count_call(start, lists, got, own):
+def count_call(table, rows, own):
     vmem = pl.BlockSpec(memory_space=pltpu.VMEM)
     return pl.pallas_call(
         count_kernel,
         out_shape=jax.ShapeDtypeStruct((SUBREGIONS, 32, 256), F32),
-        in_specs=[pl.BlockSpec(memory_space=pltpu.SMEM), vmem, vmem, vmem],
+        in_specs=[vmem, vmem, vmem],
         out_specs=vmem,
-        scratch_shapes=[
-            pltpu.VMEM((DUMMY + 1, 8, 128), F32),
-            pltpu.VMEM((32, 256), jnp.int32),
-            pltpu.SMEM((32, 256), jnp.int32),
-            pltpu.SemaphoreType.DMA,
-        ],
-        compiler_params=pltpu.CompilerParams(vmem_limit_bytes=8 << 20),
-    )(start, lists, got, own)
-
-
-MESH = pl.DeviceIdType.MESH
-
-
-def halo_kernel(lists_ref, got_ref, send_sem, recv_sem):
-    shell, sky = lax.axis_index("shell"), lax.axis_index("sky")
-    shells, skies = lax.axis_size("shell"), lax.axis_size("sky")
-    barrier = pltpu.get_barrier_semaphore()
-
-    def present(da, db):
-        a, b = shell + da, sky + db
-        return (a >= 0) & (a < shells) & (b >= 0) & (b < skies)
-
-    for da, db in DIRS:
-
-        @pl.when(present(da, db))
-        def _():
-            pl.semaphore_signal(barrier, inc=1, device_id=(shell + da, sky + db), device_id_type=MESH)
-
-    for d, (da, db) in enumerate(DIRS):
-
-        @pl.when(jnp.logical_not(present(da, db)))
-        def _():
-            got_ref[d] = jnp.zeros((4, PART_DEV), F32)
-
-    beside_shell = 1 + (shell > 0).astype(jnp.int32) + (shell < shells - 1).astype(jnp.int32)
-    beside_sky = 1 + (sky > 0).astype(jnp.int32) + (sky < skies - 1).astype(jnp.int32)
-    pl.semaphore_wait(barrier, beside_shell * beside_sky - 1)
-
-    def copy(d):
-        da, db = DIRS[d]
-        return pltpu.make_async_remote_copy(
-            src_ref=lists_ref.at[d],
-            dst_ref=got_ref.at[7 - d],
-            send_sem=send_sem.at[d],
-            recv_sem=recv_sem.at[7 - d],
-            device_id=(shell + da, sky + db),
-            device_id_type=MESH,
-        )
-
-    for d, (da, db) in enumerate(DIRS):
-
-        @pl.when(present(da, db))
-        def _():
-            copy(d).start()
-
-    for d, (da, db) in enumerate(DIRS):
-
-        @pl.when(present(da, db))
-        def _():
-            copy(d).wait_send()
-
-        @pl.when(present(-da, -db))
-        def _():
-            copy(d).wait_recv()
-
-
-def halo_call(lists):
-    return pl.pallas_call(
-        halo_kernel,
-        out_shape=jax.ShapeDtypeStruct((8, 4, PART_DEV), F32),
-        in_specs=[pl.BlockSpec(memory_space=pltpu.VMEM)],
-        out_specs=pl.BlockSpec(memory_space=pltpu.VMEM),
-        scratch_shapes=[pltpu.SemaphoreType.DMA((8,)), pltpu.SemaphoreType.DMA((8,))],
-        compiler_params=pltpu.CompilerParams(collective_id=0, has_side_effects=True, vmem_limit_bytes=4 << 20),
-    )(lists)
+        scratch_shapes=[pltpu.SMEM((GROUPS + 8, 128), jnp.int32), pltpu.SemaphoreType.DMA],
+        compiler_params=pltpu.CompilerParams(vmem_limit_bytes=6 << 20),
+    )(table, rows, own)
 
 
 def total_kernel(skies, counts_ref, own_ref, total_ref, sent_ref, land_ref, send_sem, recv_sem):
@@ -410,15 +404,18 @@
         pl.semaphore_signal(barrier, inc=1, device_id=(shell, lax.rem(sky + k, skies)), device_id_type=MESH)
     lane_in = lax.broadcasted_iota(jnp.int32, (256, 128), 0)
     lane_out = lax.broadcasted_iota(jnp.int32, (256, 128), 1)
-    packed = jnp.zeros((8 * SUBREGIONS, 128), F32)
-    for k in range(4):
-        rows = jnp.concatenate([counts_ref[r, 8 * k : 8 * k + 8, :] for r in range(SUBREGIONS)], axis=0)
-        pick = jnp.where((lane_in >> 3) + 32 * k == lane_out, 1.0, 0.0)
-        packed = packed + jnp.dot(rows, pick, precision=lax.Precision.HIGHEST, preferred_element_type=F32)
-    own_ref[...] = packed
-    mine = packed[0:8]
+    every = counts_ref[0]
     for r in range(1, SUBREGIONS):
-        mine = mine + packed[8 * r : 8 * r + 8]
+        every = every + counts_ref[r]
+    picks = [jnp.where((lane_in >> 3) + 32 * k == lane_out, 1.0, 0.0) for k in range(4)]
+
+    def pack(rows):
+        packed = jnp.dot(rows[0], picks[0], precision=lax.Precision.HIGHEST, preferred_element_type=F32)
+        for k in range(1, 4):
+            packed = packed + jnp.dot(rows[k], picks[k], precision=lax.Precision.HIGHEST, preferred_element_type=F32)
+        return packed
+
+    mine = pack([every[8 * k : 8 * k + 8] for k in range(4)])
     sent_ref[...] = mine
     pl.semaphore_wait(barrier, skies - 1)
 
@@ -434,6 +431,7 @@
 
     for k in range(1, skies):
         copy(k).start()
+    own_ref[...] = pack([jnp.concatenate([counts_ref[r, 8 * k : 8 * k + 8, :] for r in range(SUBREGIONS)], axis=0) for k in range(4)])
     total = mine
     for k in range(1, skies):
         copy(k).wait_recv()
@@ -481,8 +479,7 @@
 
 
 def local(coords, weights, live):
-    lists, own, start = sort_call(coords, weights, live)
-    counts = count_call(start, lists, halo_call(lists), own)
+    counts = count_call(*send_call(coords, weights, live))
     packed, total = total_call(counts)
     leave = total[None] - packed.reshape(SUBREGIONS, 8, 128)
     return (unpacked(leave) * bin_scale(lax.axis_size("sky"))[None, :])[None]

time: 48 us -> 42 us (0.88); the launches traced: 48 us -> 41.3 us
  Pallas kernels: 44.3 us -> 38.2 us
  local copies, waits for them, and re-layouts: 2.37 us -> 1.78 us
    pallas_call x1, Pallas kernels: 16.6 us -> 13.3 us  [count_call(): pl.pallas_call(count_kernel, out_shape=jax.ShapeDtypeStruct((SUBREGIONS,...]
    pallas_call x1, Pallas kernels: 14.7 us -> 12.7 us  [total_call(): pl.pallas_call(functools.partial(total_kernel, skies), out_shape=(jax.Sha...]
    pallas_call x2 -> x1, Pallas kernels: 13 us -> 12.2 us  [send_call(): pl.pallas_call(send_kernel, out_shape=(jax.ShapeDtypeStruct((GROUPS + 8,...]
    unnamed x6, local copies, waits for them, and re-layouts: 1.96 us -> 1.37 us
where the time goes in v3:
time: 42 us; the launch traced here: 41.3 us
  Pallas kernels  38.2 us (91%)
  local copies, waits for them, and re-layouts  1.78 us (4%)
  between operations  0.72 us (2%)
  other arithmetic  0.62 us (1%)
    pallas_call x1, Pallas kernels, count_call(): pl.pallas_call(count_kernel, out_shape=jax.ShapeDtypeStruct((SUBREGIONS,...  13.3 us
    pallas_call x1, Pallas kernels, total_call(): pl.pallas_call(functools.partial(total_kernel, skies), out_shape=(jax.Sha...  12.7 us
    pallas_call x1, Pallas kernels, send_call(): pl.pallas_call(send_kernel, out_shape=(jax.ShapeDtypeStruct((GROUPS + 8,...  12.2 us
    unnamed x6, local copies, waits for them, and re-layouts  1.37 us

profile of v3, /device:TPU:2, one launch (start us, length us, event | category | flops | bytes accessed | tf_op | source)
XLA Modules:
  0.0 41.3 jit_solution(16686162709913007217)
XLA Ops:
  0.7 0.0 copy-start
  0.7 0.7 %copy-done = s32[3,1,1,512]{3,2,1,0:T(1,128)S(1)} copy-done((s32[3,1,1,512]{3,2,1,0:T(1,128)S(1)}, s32[3,1,1,512]{3,2,1,0:T(1,128)}, u32[]{:S(2)}) %copy-start) | copy-done | bytes 6168
  1.3 0.0 copy-start.1
  1.3 0.7 %copy-done.1 = bf16[1,1,512]{2,1,0:T(2,128)(2,1)S(1)} copy-done((bf16[1,1,512]{2,1,0:T(2,128)(2,1)S(1)}, bf16[1,1,512]{2,1,0:T(2,128)(2,1)}, u32[]{:S(2)}) %copy-start.1) | copy-done | bytes 1048
  2.0 12.2 %shard_map.46 = (s32[32,128]{1,0:T(8,128)S(1)}, f32[289,8,128]{2,1,0:T(8,128)S(1)}, f32[4,24,8,128]{3,2,1,0:T(8,128)S(1)}) custom-call(s32[3,1,1,512]{3,2,1,0:T(1,128)S(1)} %copy-done, bf16[1,1,512]{2,1,0:T(2,128)(2,1)S(1)} %copy-done.1, s32[1,1]{1,0:T(1,128)S(6)} %copy.13.live_hbm), custom_call_target="tpu_custom_call" | custom-call | tf_op jit(solution)/shard_map/pallas_call | solution.py:247
  14.2 0.0 copy-start.2
  14.2 13.3 %shard_map.47.counts_ref = f32[8,32,256]{2,1,0:T(8,128)S(1)} custom-call(s32[32,128]{1,0:T(8,128)S(1)} %get-tuple-element.10.table_ref, f32[289,8,128]{2,1,0:T(8,128)S(1)} %get-tuple-element.11.rows_ref, f32[4,24,8,128]{3,2,1,0:T(8,128)S(1)} %get-tuple-element.12.own_ref), custom_call_target="tpu_custom_call" | custom-call | tf_op jit(solution)/shard_map/pallas_call | solution.py:390
  27.5 12.7 %shard_map.48 = (f32[64,128]{1,0:T(8,128)S(1)}, f32[8,128]{1,0:T(8,128)S(1)}) custom-call(f32[8,32,256]{2,1,0:T(8,128)S(1)} %shard_map.47.counts_ref), custom_call_target="tpu_custom_call" | custom-call | tf_op jit(solution)/shard_map/pallas_call | solution.py:447
  40.2 0.1 sub.11
  40.3 0.1 reshape.46
  40.5 0.1 copy.9
  40.6 0.1 reshape.48
  40.7 0.0 copy-done.2
  40.7 0.6 %broadcast_multiply_fusion = f32[1,8,600]{2,1,0:T(8,128)} fusion(f32[1,8,600]{2,1,0:T(8,128)S(1)} %reshape.48, f32[600]{0:T(1024)S(1)} %copy-done.2), kind=kLoop, calls=%fused_computation.2 | loop fusion | flops 4800 | bytes 40800 | tf_op jit(solution)/shard_map/mul | solution.py:485
  (2 shorter events, 0.0 us)
Async XLA Ops:
  0.7 0.7 %copy-start = (s32[3,1,1,512]{3,2,1,0:T(1,128)S(1)}, s32[3,1,1,512]{3,2,1,0:T(1,128)}, u32[]{:S(2)}) copy-start(s32[3,1,1,512]{3,2,1,0:T(1,128)} %coords_hbm.1) | copy-start | bytes 18436
  1.3 0.7 %copy-start.1 = (bf16[1,1,512]{2,1,0:T(2,128)(2,1)S(1)}, bf16[1,1,512]{2,1,0:T(2,128)(2,1)}, u32[]{:S(2)}) copy-start(bf16[1,1,512]{2,1,0:T(2,128)(2,1)} %weight_hbm.1) | copy-start | bytes 3076
  14.2 26.5 %copy-start.2 = (f32[600]{0:T(1024)S(1)}, f32[600]{0:T(1024)}, u32[]{:S(2)}) copy-start(f32[600]{0:T(1024)} %constant.2.clone) | copy-start | bytes 7204

commit v4 on v3

--- a/solution.py
+++ b/solution.py
@@ -214,15 +214,16 @@
             for k in range(16):
                 rows_ref[ROWS * d + 2 * k] = parts[k]
                 rows_ref[ROWS * d + 2 * k + 1] = jnp.where((lane8 & 31) < 16, turned[k], turned[k + 1])
-        batches = jnp.floor((total + (TILES - 1.0)) * (1.0 / TILES))
+        units = jnp.floor((total + 1.0) * 0.5)
         name = lax.broadcasted_iota(jnp.int32, (GROUPS, 128), 0).astype(F32)
-        number = jnp.sum(jnp.where((name >= begin) & (name < end), batches, 0.0), axis=0, keepdims=True)
-        extra = number - 2.0 * jnp.floor(number * 0.5)
-        batches = batches + jnp.sum(jnp.where(name == end - 1.0, extra, 0.0), axis=1, keepdims=True)
-        table = jnp.where(lane == 127, batches, even + 512.0 * odd)
+        number = jnp.sum(jnp.where((name >= begin) & (name < end), units, 0.0), axis=0, keepdims=True)
+        turns = jnp.floor((number + 3.0) * 0.25)
+        extra = 4.0 * turns - number
+        units = units + jnp.sum(jnp.where(name == end - 1.0, extra, 0.0), axis=1, keepdims=True)
+        table = jnp.where(lane == 127, units, even + 512.0 * odd)
         table_ref[0:GROUPS, :] = table.astype(jnp.int32)
         idle = jnp.where(lane_row == 127, float(1 << 20), float(DUMMY * 513))
-        trips = jnp.where(lane_row == SUBREGIONS, starts[SUBREGIONS], (number + extra) * 0.5)
+        trips = jnp.where(lane_row == SUBREGIONS, starts[SUBREGIONS], turns)
         tail = jnp.concatenate([idle, trips, jnp.zeros((6, 128), F32)], axis=0)
         table_ref[GROUPS : GROUPS + 8, :] = tail.astype(jnp.int32)
         for d, (da, db) in enumerate(DIRS):
@@ -264,7 +265,7 @@
             pltpu.SemaphoreType.DMA((8,)),
         ],
         compiler_params=pltpu.CompilerParams(collective_id=0, has_side_effects=True, vmem_limit_bytes=12 << 20),
-    )(coords, weights, live)
+    )(*[pltpu.with_memory_space_constraint(v, pltpu.HBM) for v in (coords, weights)], live)
 
 
 LOG_SCALE = (S_BINS / 4.0) / math.log2(10.0)
@@ -291,36 +292,36 @@
         def index(state):
             g, b = state
             for half in range(2):
-                group = jnp.minimum(g, GROUPS - 1)
-                xi, yi, zi, wi = own_ref[0, group], own_ref[1, group], own_ref[2, group], own_ref[3, group]
-                own_w[half] = jnp.concatenate([wi, wi], axis=0).astype(BF16)
-                for t in range(TILES):
-                    pair = table_sm[g, TILES // 2 * b + t // 2]
-                    row = pair & 511 if t % 2 == 0 else pair >> 9
-                    dx = xi - rows_ref[row, 0:1, :]
-                    dy = yi - rows_ref[row, 1:2, :]
-                    dz = zi - rows_ref[row, 2:3, :]
-                    far_w[half, t] = jnp.broadcast_to(rows_ref[row, 3:4, :].astype(BF16), (16, 128))
-                    dx2 = dx * dx
-                    q = dx2 + dy * dy + dz * dz
-                    s = jnp.floor(jnp.log2(q + 0.48) * LOG_SCALE + LOG_BASE)
-                    near = jnp.floor(jnp.abs(dx) * lax.rsqrt(q) * float(MU_BINS) + 0.5)
-                    mu = jnp.where(near * near * q > dx2 * float(MU_BINS * MU_BINS), near - 1.0, near)
-                    c = s * float(MU_BINS) + jnp.minimum(mu, MU_BINS - 1.0)
-                    u = jnp.floor(c * (1.0 / LEVELS_V) + 0.01)
-                    v = c - u * float(LEVELS_V)
-                    bin_u[half, t] = jnp.concatenate([u, u - 1.0], axis=0).astype(BF16)
-                    bin_v[half, t] = jnp.concatenate([v, v - 1.0], axis=0).astype(BF16)
-                b = b + 1
-                over = b >= table_sm[g, 127]
-                g = jnp.where(over, g + 1, g)
-                g = jnp.where(g >= stop, GROUPS, g)
-                b = jnp.where(over, 0, b)
+                for mxu in range(2):
+                    group = jnp.minimum(g, GROUPS - 1)
+                    xi, yi, zi, wi = own_ref[0, group], own_ref[1, group], own_ref[2, group], own_ref[3, group]
+                    own_w[half, mxu] = jnp.concatenate([wi, wi], axis=0).astype(BF16)
+                    pair = table_sm[g, b]
+                    for t, row in ((2 * mxu, pair & 511), (2 * mxu + 1, pair >> 9)):
+                        dx = xi - rows_ref[row, 0:1, :]
+                        dy = yi - rows_ref[row, 1:2, :]
+                        dz = zi - rows_ref[row, 2:3, :]
+                        far_w[half, t] = jnp.broadcast_to(rows_ref[row, 3:4, :].astype(BF16), (16, 128))
+                        dx2 = dx * dx
+                        q = dx2 + dy * dy + dz * dz
+                        s = jnp.floor(jnp.log2(q + 0.48) * LOG_SCALE + LOG_BASE)
+                        near = jnp.floor(jnp.abs(dx) * lax.rsqrt(q) * float(MU_BINS) + 0.5)
+                        mu = jnp.where(near * near * q > dx2 * float(MU_BINS * MU_BINS), near - 1.0, near)
+                        c = s * float(MU_BINS) + jnp.minimum(mu, MU_BINS - 1.0)
+                        u = jnp.floor(c * (1.0 / LEVELS_V) + 0.01)
+                        v = c - u * float(LEVELS_V)
+                        bin_u[half, t] = jnp.concatenate([u, u - 1.0], axis=0).astype(BF16)
+                        bin_v[half, t] = jnp.concatenate([v, v - 1.0], axis=0).astype(BF16)
+                    b = b + 1
+                    over = b >= table_sm[g, 127]
+                    g = jnp.where(over, g + 1, g)
+                    g = jnp.where(g >= stop, GROUPS, g)
+                    b = jnp.where(over, 0, b)
             return g, b
 
         def fill(half):
-            w_own = own_w[half]
             for t in range(TILES):
+                w_own = own_w[half, t // 2]
                 u2, v2, w_far = bin_u[half, t], bin_v[half, t], far_w[half, t]
                 lanes = slice(128 * t, 128 * t + 128)
                 for k in range(LEVELS_U // 2):
@@ -342,15 +343,9 @@
             fill(half)
             push(half)
         state = index(state)
-        sub = lax.broadcasted_iota(jnp.int32, (8, 256), 0)
-        diagonal = sub == (lax.broadcasted_iota(jnp.int32, (8, 256), 1) & 7)
-
         def drain(r):
             accs = sets[r % 2]
-            both = pltpu.matmul_pop(accs[0]) + pltpu.matmul_pop(accs[1])
-            for v in range(V_ROWS // 8):
-                out_ref[r, v : v + 1, :] = jnp.sum(jnp.where(diagonal, both[8 * v : 8 * v + 8], 0.0), axis=0, keepdims=True)
-            out_ref[r, V_ROWS // 8 :, :] = jnp.zeros((32 - V_ROWS // 8, 256), F32)
+            out_ref[r] = pltpu.matmul_pop(accs[0]) + pltpu.matmul_pop(accs[1])
 
         for r in range(SUBREGIONS):
             accs = sets[r % 2]
@@ -381,7 +376,7 @@
         pltpu.VMEM((2, TILES, 16, 128), BF16),
         pltpu.VMEM((2, TILES, 16, 128), BF16),
         pltpu.VMEM((2, TILES, 16, 128), BF16),
-        pltpu.VMEM((2, 16, 128), BF16),
+        pltpu.VMEM((2, 2, 16, 128), BF16),
     )
 
 
@@ -389,7 +384,7 @@
     vmem = pl.BlockSpec(memory_space=pltpu.VMEM)
     return pl.pallas_call(
         count_kernel,
-        out_shape=jax.ShapeDtypeStruct((SUBREGIONS, 32, 256), F32),
+        out_shape=jax.ShapeDtypeStruct((SUBREGIONS, V_ROWS, 256), F32),
         in_specs=[vmem, vmem, vmem],
         out_specs=vmem,
         scratch_shapes=[pltpu.SMEM((GROUPS + 8, 128), jnp.int32), pltpu.SemaphoreType.DMA],
@@ -404,10 +399,12 @@
         pl.semaphore_signal(barrier, inc=1, device_id=(shell, lax.rem(sky + k, skies)), device_id_type=MESH)
     lane_in = lax.broadcasted_iota(jnp.int32, (256, 128), 0)
     lane_out = lax.broadcasted_iota(jnp.int32, (256, 128), 1)
-    every = counts_ref[0]
-    for r in range(1, SUBREGIONS):
-        every = every + counts_ref[r]
     picks = [jnp.where((lane_in >> 3) + 32 * k == lane_out, 1.0, 0.0) for k in range(4)]
+    diagonal = lax.broadcasted_iota(jnp.int32, (V_ROWS, 256), 0) & 7 == lax.broadcasted_iota(jnp.int32, (V_ROWS, 256), 1) & 7
+
+    def folded(block):
+        block = jnp.where(diagonal, block, 0.0).reshape(V_ROWS // 8, 8, 256)
+        return jnp.concatenate([jnp.sum(block, axis=1), jnp.zeros((32 - V_ROWS // 8, 256), F32)], axis=0)
 
     def pack(rows):
         packed = jnp.dot(rows[0], picks[0], precision=lax.Precision.HIGHEST, preferred_element_type=F32)
@@ -415,6 +412,10 @@
             packed = packed + jnp.dot(rows[k], picks[k], precision=lax.Precision.HIGHEST, preferred_element_type=F32)
         return packed
 
+    every = counts_ref[0]
+    for r in range(1, SUBREGIONS):
+        every = every + counts_ref[r]
+    every = folded(every)
     mine = pack([every[8 * k : 8 * k + 8] for k in range(4)])
     sent_ref[...] = mine
     pl.semaphore_wait(barrier, skies - 1)
@@ -431,7 +432,8 @@
 
     for k in range(1, skies):
         copy(k).start()
-    own_ref[...] = pack([jnp.concatenate([counts_ref[r, 8 * k : 8 * k + 8, :] for r in range(SUBREGIONS)], axis=0) for k in range(4)])
+    each = [folded(counts_ref[r]) for r in range(SUBREGIONS)]
+    own_ref[...] = pack([jnp.concatenate([block[8 * k : 8 * k + 8] for block in each], axis=0) for k in range(4)])
     total = mine
     for k in range(1, skies):
         copy(k).wait_recv()

time: 42 us -> 40 us (0.952)
  the two profiles are of different devices: /device:TPU:2 before, /device:TPU:36 now
where the time goes in v4:
time: 40 us; the launch traced here: 40.5 us
  Pallas kernels  38.7 us (97%)
  between operations  0.71 us (2%)
  other arithmetic  0.62 us (2%)
  local copies, waits for them, and re-layouts  0.42 us (1%)
    pallas_call x1, Pallas kernels, total_call(): pl.pallas_call(functools.partial(total_kernel, skies), out_shape=(jax.Sha...  22.8 us
    pallas_call x1, Pallas kernels, send_call(): pl.pallas_call(send_kernel, out_shape=(jax.ShapeDtypeStruct((GROUPS + 8,...  11.4 us
    pallas_call x1, Pallas kernels, count_call(): pl.pallas_call(count_kernel, out_shape=jax.ShapeDtypeStruct((SUBREGIONS,...  4.48 us

profile of v4, /device:TPU:36, one launch (start us, length us, event | category | flops | bytes accessed | tf_op | source)
XLA Modules:
  0.0 40.5 jit_solution(10000814473385187206)
XLA Ops:
  0.7 11.4 %shard_map.46 = (s32[32,128]{1,0:T(8,128)S(1)}, f32[289,8,128]{2,1,0:T(8,128)S(1)}, f32[4,24,8,128]{3,2,1,0:T(8,128)S(1)}) custom-call(s32[3,1,1,512]{3,2,1,0:T(1,128)} %coords_hbm.1, bf16[1,1,512]{2,1,0:T(2,128)(2,1)} %weight_hbm.1, s32[1,1]{1,0:T(1,128)S(6)} %copy.13.live_hbm), custom_call_target="tpu_custom_call" | custom-call | tf_op jit(solution)/shard_map/pallas_call | solution.py:248
  12.1 4.5 %shard_map.47.counts_ref = f32[8,208,256]{2,1,0:T(8,128)S(1)} custom-call(s32[32,128]{1,0:T(8,128)S(1)} %get-tuple-element.10.table_ref, f32[289,8,128]{2,1,0:T(8,128)S(1)} %get-tuple-element.11.rows_ref, f32[4,24,8,128]{3,2,1,0:T(8,128)S(1)} %get-tuple-element.12.own_ref), custom_call_target="tpu_custom_call" | custom-call | tf_op jit(solution)/shard_map/pallas_call | solution.py:385
  16.6 0.0 copy-start
  16.6 22.8 %shard_map.48 = (f32[64,128]{1,0:T(8,128)S(1)}, f32[8,128]{1,0:T(8,128)S(1)}) custom-call(f32[8,208,256]{2,1,0:T(8,128)S(1)} %shard_map.47.counts_ref), custom_call_target="tpu_custom_call" | custom-call | tf_op jit(solution)/shard_map/pallas_call | solution.py:449
  39.4 0.1 sub.11
  39.5 0.1 reshape.46
  39.7 0.1 copy.9
  39.8 0.1 reshape.48
  39.9 0.0 copy-done
  39.9 0.6 %broadcast_multiply_fusion = f32[1,8,600]{2,1,0:T(8,128)} fusion(f32[1,8,600]{2,1,0:T(8,128)S(1)} %reshape.48, f32[600]{0:T(1024)S(1)} %copy-done), kind=kLoop, calls=%fused_computation.2 | loop fusion | flops 4800 | bytes 40800 | tf_op jit(solution)/shard_map/mul | solution.py:487
  (2 shorter events, 0.0 us)
Async XLA Ops:
  16.6 23.3 %copy-start = (f32[600]{0:T(1024)S(1)}, f32[600]{0:T(1024)}, u32[]{:S(2)}) copy-start(f32[600]{0:T(1024)} %constant.2.clone) | copy-start | bytes 7204

commit v5 on v4

--- a/solution.py
+++ b/solution.py
@@ -12,6 +12,7 @@
 S_BINS = 30
 MU_BINS = 20
 REACH = 199
+CLOSE = 43
 GROUPS = 24
 STEP = 16
 ROWS = PART_DEV // STEP
@@ -102,16 +103,21 @@
             pltpu.matmul_acc_lhs(acc1, flags[:, rows], load_staged_rhs=0)
         rank = jnp.concatenate([pltpu.matmul_pop(acc0), pltpu.matmul_pop(acc1)], axis=1)
         attrs = jnp.concatenate([x, y, z_high, z_low, w, jnp.zeros((11, n), F32)], axis=0).astype(BF16)
-        place = lax.broadcasted_iota(jnp.int32, (n, 1), 0).astype(F32)
+        place = lax.broadcasted_iota(jnp.int32, (256, n), 0).astype(F32).astype(BF16)
+        one, zero = jnp.ones((256, n), BF16), jnp.zeros((256, n), BF16)
         accs = ((acc0, acc1), (acc2, acc3))
-        for d in range(9):
+        beside_shell = 1 + (shell > 0).astype(jnp.int32) + (shell < shells - 1).astype(jnp.int32)
+        beside_sky = 1 + (sky > 0).astype(jnp.int32) + (sky < skies - 1).astype(jnp.int32)
+
+        def build(d):
             target = jnp.where(valid[d], rank[d : d + 1, :], -1.0)
-            hot = jnp.where(place == target, 1.0, 0.0).astype(BF16)
             pair = accs[d % 2]
-            for half in range(2):
-                cols = slice(256 * half, 256 * half + 256)
-                for mxu in range(2):
-                    pltpu.matmul_push_rhs(hot[256 * mxu : 256 * mxu + 256, cols], staging_register=0, mxu_index=mxu, transpose=True)
+            for mxu in range(2):
+                near = jnp.broadcast_to((target - 256.0 * mxu).astype(BF16), (256, n))
+                hot = jnp.where(place == near, one, zero)
+                for half in range(2):
+                    cols = slice(256 * half, 256 * half + 256)
+                    pltpu.matmul_push_rhs(hot[:, cols], staging_register=0, mxu_index=mxu, transpose=True)
                     pltpu.matmul_acc_lhs(pair[mxu], attrs[:, cols], load_staged_rhs=0)
             da, db = DIRS[d] if d < 8 else (0, 0)
             for mxu in range(2):
@@ -122,12 +128,12 @@
                 lists_ref[d, 2:3, lanes] = got[2:3] * 128.0 + got[3:4]
                 lists_ref[d, 3:4, lanes] = got[4:5]
 
-        beside_shell = 1 + (shell > 0).astype(jnp.int32) + (shell < shells - 1).astype(jnp.int32)
-        beside_sky = 1 + (sky > 0).astype(jnp.int32) + (sky < skies - 1).astype(jnp.int32)
+        for d in range(9):
+            build(d)
         pl.semaphore_wait(barrier, beside_shell * beside_sky - 1)
-        for d, (da, db) in enumerate(DIRS):
-
-            @pl.when(present(da, db))
+        for d in (0, 2, 5, 7, 3, 4, 1, 6):
+
+            @pl.when(present(*DIRS[d]))
             def _():
                 copy(d).start()
 
@@ -178,9 +184,8 @@
         z_max = jnp.max(jnp.max(jnp.where(ws > 0.0, zs, -1e6), axis=1), axis=1, keepdims=True)
         lane = lax.broadcasted_iota(jnp.int32, (GROUPS, 128), 1)
         chunk = lane.astype(F32) * 2.0
-        even = jnp.full((GROUPS, 128), float(DUMMY), F32)
-        odd = even
-        total = jnp.zeros((GROUPS, 1), F32)
+        near_even = near_odd = far_even = far_odd = jnp.full((GROUPS, 128), float(DUMMY), F32)
+        near_total = far_total = jnp.zeros((GROUPS, 1), F32)
         lane8 = lax.broadcasted_iota(jnp.int32, (8, 128), 1)
         rows_ref[DUMMY] = jnp.zeros((8, 128), F32)
         for d in (8, 3, 4, 1, 6, 0, 2, 5, 7):
@@ -192,15 +197,30 @@
 
             src = lists_ref.at[8] if d == 8 else got_ref.at[d]
             z_row = jnp.where(src[3:4, :] > 0.0, src[2:3, :], 2e6)
-            low = jnp.sum(jnp.where(z_row < z_min - float(REACH), 1.0, 0.0), axis=1, keepdims=True)
-            high = jnp.sum(jnp.where(z_row <= z_max + float(REACH), 1.0, 0.0), axis=1, keepdims=True)
+            below = lambda edge: jnp.sum(jnp.where(z_row < edge, 1.0, 0.0), axis=1, keepdims=True)
+            low, high = below(z_min - float(REACH)), below(z_max + float(REACH + 1))
             first = jnp.floor(low * (1.0 / STEP))
-            count = jnp.where(high > low, jnp.floor((high - STEP * first + 31.0) * (1.0 / 32.0)), 0.0)
-            at = chunk - total
-            even = jnp.where((at >= 0.0) & (at < count), at * 2.0 + (first + float(ROWS * d)), even)
-            at = at + 1.0
-            odd = jnp.where((at >= 0.0) & (at < count), at * 2.0 + (first + float(ROWS * d)), odd)
-            total = total + count
+            base = STEP * first
+            count = jnp.where(high > low, jnp.floor((high - base + 31.0) * (1.0 / 32.0)), 0.0)
+            head = jnp.floor((below(z_min - float(CLOSE)) - base) * (1.0 / 32.0))
+            head = jnp.minimum(jnp.maximum(head, 0.0), count)
+            rest = jnp.floor((below(z_max + float(CLOSE + 1)) - base + 31.0) * (1.0 / 32.0))
+            rest = jnp.minimum(jnp.maximum(rest, head), count)
+            middle = rest - head
+            start = first + float(ROWS * d)
+
+            def near_put(at, table):
+                return jnp.where((at >= 0.0) & (at < middle), (at + head) * 2.0 + start, table)
+
+            def far_put(at, table):
+                return jnp.where((at >= 0.0) & (at < count - middle), (at + jnp.where(at >= head, middle, 0.0)) * 2.0 + start, table)
+
+            near_even = near_put(chunk - near_total, near_even)
+            near_odd = near_put(chunk + 1.0 - near_total, near_odd)
+            far_even = far_put(chunk - far_total, far_even)
+            far_odd = far_put(chunk + 1.0 - far_total, far_odd)
+            near_total = near_total + middle
+            far_total = far_total + (count - middle)
             parts = []
             for t in range(4):
                 block = src[:, 128 * t : 128 * t + 128]
@@ -214,18 +234,21 @@
             for k in range(16):
                 rows_ref[ROWS * d + 2 * k] = parts[k]
                 rows_ref[ROWS * d + 2 * k + 1] = jnp.where((lane8 & 31) < 16, turned[k], turned[k + 1])
-        units = jnp.floor((total + 1.0) * 0.5)
         name = lax.broadcasted_iota(jnp.int32, (GROUPS, 128), 0).astype(F32)
-        number = jnp.sum(jnp.where((name >= begin) & (name < end), units, 0.0), axis=0, keepdims=True)
-        turns = jnp.floor((number + 3.0) * 0.25)
-        extra = 4.0 * turns - number
-        units = units + jnp.sum(jnp.where(name == end - 1.0, extra, 0.0), axis=1, keepdims=True)
-        table = jnp.where(lane == 127, units, even + 512.0 * odd)
-        table_ref[0:GROUPS, :] = table.astype(jnp.int32)
         idle = jnp.where(lane_row == 127, float(1 << 20), float(DUMMY * 513))
-        trips = jnp.where(lane_row == SUBREGIONS, starts[SUBREGIONS], turns)
-        tail = jnp.concatenate([idle, trips, jnp.zeros((6, 128), F32)], axis=0)
-        table_ref[GROUPS : GROUPS + 8, :] = tail.astype(jnp.int32)
+
+        def finish(units, even, odd):
+            number = jnp.sum(jnp.where((name >= begin) & (name < end), units, 0.0), axis=0, keepdims=True)
+            turns = jnp.floor((number + 3.0) * 0.25)
+            extra = 4.0 * turns - number
+            units = units + jnp.sum(jnp.where(name == end - 1.0, extra, 0.0), axis=1, keepdims=True)
+            return jnp.where(lane == 127, units, even + 512.0 * odd), turns
+
+        near_table, near_turns = finish(jnp.floor((near_total + 1.0) * 0.5), near_even, near_odd)
+        far_table, far_turns = finish(jnp.maximum(jnp.floor((far_total + 3.0) * 0.25), 1.0), far_even, far_odd)
+        far_turns = jnp.where(lane_row == SUBREGIONS, starts[SUBREGIONS], far_turns)
+        pad = jnp.zeros((6, 128), F32)
+        table_ref[...] = jnp.concatenate([near_table, idle, near_turns, pad, far_table, idle, far_turns, pad], axis=0).astype(jnp.int32)
         for d, (da, db) in enumerate(DIRS):
 
             @pl.when(present(da, db))
@@ -248,7 +271,7 @@
     return pl.pallas_call(
         send_kernel,
         out_shape=(
-            jax.ShapeDtypeStruct((GROUPS + 8, 128), jnp.int32),
+            jax.ShapeDtypeStruct((2 * GROUPS + 16, 128), jnp.int32),
             jax.ShapeDtypeStruct((DUMMY + 1, 8, 128), F32),
             jax.ShapeDtypeStruct((4, GROUPS, 8, 128), F32),
         ),
@@ -272,6 +295,9 @@
 LOG_BASE = -4.515457845
 LEVELS_U = 24
 LEVELS_V = 25
+FAR_FIRST = 400
+FAR_U = 16
+FAR_V = 13
 V_ROWS = 208
 
 
@@ -285,50 +311,63 @@
         for half in range(2):
             hot_u[half, 8 * LEVELS_U :, :] = jnp.zeros((256 - 8 * LEVELS_U, 128 * TILES), BF16)
         copy.wait()
-        trips = [table_sm[GROUPS + 1, r] for r in range(SUBREGIONS)]
-        stop = table_sm[GROUPS + 1, SUBREGIONS]
+        stop = table_sm[2 * GROUPS + 9, SUBREGIONS]
         zero = jnp.zeros((16, 128), BF16)
 
-        def index(state):
-            g, b = state
-            for half in range(2):
-                for mxu in range(2):
-                    group = jnp.minimum(g, GROUPS - 1)
-                    xi, yi, zi, wi = own_ref[0, group], own_ref[1, group], own_ref[2, group], own_ref[3, group]
-                    own_w[half, mxu] = jnp.concatenate([wi, wi], axis=0).astype(BF16)
-                    pair = table_sm[g, b]
-                    for t, row in ((2 * mxu, pair & 511), (2 * mxu + 1, pair >> 9)):
-                        dx = xi - rows_ref[row, 0:1, :]
-                        dy = yi - rows_ref[row, 1:2, :]
-                        dz = zi - rows_ref[row, 2:3, :]
-                        far_w[half, t] = jnp.broadcast_to(rows_ref[row, 3:4, :].astype(BF16), (16, 128))
-                        dx2 = dx * dx
-                        q = dx2 + dy * dy + dz * dz
-                        s = jnp.floor(jnp.log2(q + 0.48) * LOG_SCALE + LOG_BASE)
-                        near = jnp.floor(jnp.abs(dx) * lax.rsqrt(q) * float(MU_BINS) + 0.5)
-                        mu = jnp.where(near * near * q > dx2 * float(MU_BINS * MU_BINS), near - 1.0, near)
-                        c = s * float(MU_BINS) + jnp.minimum(mu, MU_BINS - 1.0)
-                        u = jnp.floor(c * (1.0 / LEVELS_V) + 0.01)
-                        v = c - u * float(LEVELS_V)
-                        bin_u[half, t] = jnp.concatenate([u, u - 1.0], axis=0).astype(BF16)
-                        bin_v[half, t] = jnp.concatenate([v, v - 1.0], axis=0).astype(BF16)
-                    b = b + 1
-                    over = b >= table_sm[g, 127]
-                    g = jnp.where(over, g + 1, g)
-                    g = jnp.where(g >= stop, GROUPS, g)
-                    b = jnp.where(over, 0, b)
-            return g, b
-
-        def fill(half):
+        def combined(own, row):
+            dx = own[0] - rows_ref[row, 0:1, :]
+            dy = own[1] - rows_ref[row, 1:2, :]
+            dz = own[2] - rows_ref[row, 2:3, :]
+            dx2 = dx * dx
+            q = dx2 + dy * dy + dz * dz
+            s = jnp.floor(jnp.log2(q + 0.48) * LOG_SCALE + LOG_BASE)
+            near = jnp.floor(jnp.abs(dx) * lax.rsqrt(q) * float(MU_BINS) + 0.5)
+            mu = jnp.where(near * near * q > dx2 * float(MU_BINS * MU_BINS), near - 1.0, near)
+            return s * float(MU_BINS) + jnp.minimum(mu, MU_BINS - 1.0)
+
+        def near_unit(own, g, b, half, mxu):
+            pair = table_sm[g, b]
+            for t, row in ((2 * mxu, pair & 511), (2 * mxu + 1, pair >> 9)):
+                far_w[half, t] = jnp.broadcast_to(rows_ref[row, 3:4, :].astype(BF16), (16, 128))
+                c = combined(own, row)
+                u = jnp.floor(c * (1.0 / LEVELS_V) + 0.01)
+                v = c - u * float(LEVELS_V)
+                bin_u[half, t] = jnp.concatenate([u, u - 1.0], axis=0).astype(BF16)
+                bin_v[half, t] = jnp.concatenate([v, v - 1.0], axis=0).astype(BF16)
+
+        def far_unit(own, g, b, half, mxu):
+            for k in range(2):
+                pair = table_sm[GROUPS + 8 + g, 2 * b + k]
+                rows = (pair & 511, pair >> 9)
+                t = 2 * mxu + k
+                far_w[half, t] = jnp.concatenate([jnp.broadcast_to(rows_ref[row, 3:4, :], (8, 128)) for row in rows], axis=0).astype(BF16)
+                us, vs = [], []
+                for row in rows:
+                    c = combined(own, row) - float(FAR_FIRST)
+                    u = jnp.floor(c * (1.0 / FAR_V) + 0.01)
+                    us.append(u)
+                    vs.append(c - u * float(FAR_V))
+                bin_u[half, t] = jnp.concatenate(us, axis=0).astype(BF16)
+                bin_v[half, t] = jnp.concatenate(vs, axis=0).astype(BF16)
+
+        def near_fill(half):
             for t in range(TILES):
-                w_own = own_w[half, t // 2]
-                u2, v2, w_far = bin_u[half, t], bin_v[half, t], far_w[half, t]
+                u2, v2, w_far, w_own = bin_u[half, t], bin_v[half, t], far_w[half, t], own_w[half, t // 2]
                 lanes = slice(128 * t, 128 * t + 128)
                 for k in range(LEVELS_U // 2):
                     hot_u[half, 16 * k : 16 * k + 16, lanes] = jnp.where(u2 == jnp.bfloat16(2 * k), w_far, zero)
                 for k in range(V_ROWS // 16):
                     hot_v[half, 16 * k : 16 * k + 16, lanes] = jnp.where(v2 == jnp.bfloat16(2 * k), w_own, zero)
 
+        def far_fill(half):
+            for t in range(TILES):
+                u2, v2, w_far, w_own = bin_u[half, t], bin_v[half, t], far_w[half, t], own_w[half, t // 2]
+                lanes = slice(128 * t, 128 * t + 128)
+                for k in range(FAR_U):
+                    hot_u[half, 16 * k : 16 * k + 16, lanes] = jnp.where(u2 == jnp.bfloat16(k), w_far, zero)
+                for k in range(FAR_V):
+                    hot_v[half, 16 * k : 16 * k + 16, lanes] = jnp.where(v2 == jnp.bfloat16(k), w_own, zero)
+
         def push(half):
             for mxu in range(2):
                 pltpu.matmul_push_rhs(hot_u[half, :, 256 * mxu : 256 * mxu + 256], staging_register=half, mxu_index=mxu, transpose=True)
@@ -337,33 +376,52 @@
             for mxu in range(2):
                 pltpu.matmul_acc_lhs(accs[mxu], hot_v[half, :, 256 * mxu : 256 * mxu + 256], load_staged_rhs=half)
 
-        state = (jnp.where(stop > 0, 0, GROUPS).astype(jnp.int32), jnp.int32(0))
-        state = index(state)
-        for half in range(2):
-            fill(half)
-            push(half)
-        state = index(state)
-        def drain(r):
-            accs = sets[r % 2]
-            out_ref[r] = pltpu.matmul_pop(accs[0]) + pltpu.matmul_pop(accs[1])
-
-        for r in range(SUBREGIONS):
-            accs = sets[r % 2]
-
-            def trip(_, state):
+        def phase(unit, fill, first_row, out):
+            def index(state):
+                g, b = state
                 for half in range(2):
-                    multiply(half, accs)
-                for half in range(2):
-                    fill(half)
-                    push(half)
-                return index(state)
-
-            state = lax.fori_loop(0, trips[r], trip, state)
-            if r > 0:
-                drain(r - 1)
-        for half in range(2):
-            multiply(half, sets[(SUBREGIONS - 1) % 2])
-        drain(SUBREGIONS - 1)
+                    for mxu in range(2):
+                        group = jnp.minimum(g, GROUPS - 1)
+                        own = (own_ref[0, group], own_ref[1, group], own_ref[2, group])
+                        wi = own_ref[3, group]
+                        own_w[half, mxu] = jnp.concatenate([wi, wi], axis=0).astype(BF16)
+                        unit(own, g, b, half, mxu)
+                        b = b + 1
+                        over = b >= table_sm[first_row + g, 127]
+                        g = jnp.where(over, g + 1, g)
+                        g = jnp.where(g >= stop, GROUPS, g)
+                        b = jnp.where(over, 0, b)
+                return g, b
+
+            def drain(r):
+                accs = sets[r % 2]
+                out_ref[out + r] = pltpu.matmul_pop(accs[0]) + pltpu.matmul_pop(accs[1])
+
+            state = index((jnp.where(stop > 0, 0, GROUPS).astype(jnp.int32), jnp.int32(0)))
+            for half in range(2):
+                fill(half)
+                push(half)
+            state = index(state)
+            for r in range(SUBREGIONS):
+                accs = sets[r % 2]
+
+                def trip(_, state):
+                    for half in range(2):
+                        multiply(half, accs)
+                    for half in range(2):
+                        fill(half)
+                        push(half)
+                    return index(state)
+
+                state = lax.fori_loop(0, table_sm[first_row + GROUPS + 1, r], trip, state)
+                if r > 0:
+                    drain(r - 1)
+            for half in range(2):
+                multiply(half, sets[(SUBREGIONS - 1) % 2])
+            drain(SUBREGIONS - 1)
+
+        phase(near_unit, near_fill, 0, 0)
+        phase(far_unit, far_fill, GROUPS + 8, SUBREGIONS)
 
     pl.run_scoped(
         body,
@@ -384,11 +442,11 @@
     vmem = pl.BlockSpec(memory_space=pltpu.VMEM)
     return pl.pallas_call(
         count_kernel,
-        out_shape=jax.ShapeDtypeStruct((SUBREGIONS, V_ROWS, 256), F32),
+        out_shape=jax.ShapeDtypeStruct((2 * SUBREGIONS, V_ROWS, 256), F32),
         in_specs=[vmem, vmem, vmem],
         out_specs=vmem,
-        scratch_shapes=[pltpu.SMEM((GROUPS + 8, 128), jnp.int32), pltpu.SemaphoreType.DMA],
-        compiler_params=pltpu.CompilerParams(vmem_limit_bytes=6 << 20),
+        scratch_shapes=[pltpu.SMEM((2 * GROUPS + 16, 128), jnp.int32), pltpu.SemaphoreType.DMA],
+        compiler_params=pltpu.CompilerParams(vmem_limit_bytes=8 << 20),
     )(table, rows, own)
 
 
@@ -400,23 +458,35 @@
     lane_in = lax.broadcasted_iota(jnp.int32, (256, 128), 0)
     lane_out = lax.broadcasted_iota(jnp.int32, (256, 128), 1)
     picks = [jnp.where((lane_in >> 3) + 32 * k == lane_out, 1.0, 0.0) for k in range(4)]
-    diagonal = lax.broadcasted_iota(jnp.int32, (V_ROWS, 256), 0) & 7 == lax.broadcasted_iota(jnp.int32, (V_ROWS, 256), 1) & 7
-
-    def folded(block):
-        block = jnp.where(diagonal, block, 0.0).reshape(V_ROWS // 8, 8, 256)
-        return jnp.concatenate([jnp.sum(block, axis=1), jnp.zeros((32 - V_ROWS // 8, 256), F32)], axis=0)
-
-    def pack(rows):
-        packed = jnp.dot(rows[0], picks[0], precision=lax.Precision.HIGHEST, preferred_element_type=F32)
-        for k in range(1, 4):
-            packed = packed + jnp.dot(rows[k], picks[k], precision=lax.Precision.HIGHEST, preferred_element_type=F32)
+    level = lane_in >> 4
+    for k in range(2):
+        spot = 32 * (2 * k + (level >> 3)) + LEVELS_U + (level & 7)
+        picks.append(jnp.where(spot == lane_out, 1.0, 0.0))
+
+    def folded(block, size):
+        rows = lax.broadcasted_iota(jnp.int32, (V_ROWS, 256), 0)
+        lanes = lax.broadcasted_iota(jnp.int32, (V_ROWS, 256), 1)
+        block = jnp.where((rows & (size - 1)) == (lanes & (size - 1)), block, 0.0)
+        block = jnp.sum(block.reshape(V_ROWS // size, size, 256), axis=1)
+        full = 32 * 8 // size
+        return jnp.concatenate([block, jnp.zeros((full - V_ROWS // size, 256), F32)], axis=0)
+
+    def pack(pairs):
+        packed = None
+        for k in range(6):
+            rows = [pair[k // 4][8 * (k % 4) : 8 * (k % 4) + 8] for pair in pairs]
+            rows = rows[0] if len(rows) == 1 else jnp.concatenate(rows, axis=0)
+            part = jnp.dot(rows, picks[k], precision=lax.Precision.HIGHEST, preferred_element_type=F32)
+            packed = part if packed is None else packed + part
         return packed
 
-    every = counts_ref[0]
-    for r in range(1, SUBREGIONS):
-        every = every + counts_ref[r]
-    every = folded(every)
-    mine = pack([every[8 * k : 8 * k + 8] for k in range(4)])
+    every = []
+    for out, size in ((0, 8), (SUBREGIONS, 16)):
+        block = counts_ref[out]
+        for r in range(1, SUBREGIONS):
+            block = block + counts_ref[out + r]
+        every.append(folded(block, size))
+    mine = pack([every])
     sent_ref[...] = mine
     pl.semaphore_wait(barrier, skies - 1)
 
@@ -432,8 +502,7 @@
 
     for k in range(1, skies):
         copy(k).start()
-    each = [folded(counts_ref[r]) for r in range(SUBREGIONS)]
-    own_ref[...] = pack([jnp.concatenate([block[8 * k : 8 * k + 8] for block in each], axis=0) for k in range(4)])
+    own_ref[...] = pack([(folded(counts_ref[r], 8), folded(counts_ref[SUBREGIONS + r], 16)) for r in range(SUBREGIONS)])
     total = mine
     for k in range(1, skies):
         copy(k).wait_recv()
@@ -476,8 +545,12 @@
 
 
 def unpacked(x):
-    x = x.reshape(-1, 8, 4, 32).transpose(0, 3, 2, 1).reshape(-1, 32, 32)
-    return x[:, :LEVELS_U, :LEVELS_V].reshape(-1, S_BINS * MU_BINS)
+    x = x.reshape(-1, 8, 4, 32)
+    near = x[..., :LEVELS_U].transpose(0, 3, 2, 1).reshape(-1, LEVELS_U, 32)
+    near = near[:, :, :LEVELS_V].reshape(-1, S_BINS * MU_BINS)
+    far = x[..., LEVELS_U:].reshape(-1, 8, 2, 2, 8).transpose(0, 3, 4, 2, 1).reshape(-1, FAR_U, 16)
+    far = far[:, :, :FAR_V].reshape(-1, FAR_U * FAR_V)[:, : S_BINS * MU_BINS - FAR_FIRST]
+    return near + jnp.pad(far, ((0, 0), (FAR_FIRST, 0)))
 
 
 def local(coords, weights, live):

time: 40 us -> 41 us (1.025)
  the two profiles are of different devices: /device:TPU:36 before, /device:TPU:4 now
where the time goes in v5:
time: 41 us; the launch traced here: 41.4 us
  Pallas kernels  39.1 us (95%)
  local copies, waits for them, and re-layouts  0.85 us (2%)
  between operations  0.74 us (2%)
  other arithmetic  0.7 us (2%)
    pallas_call x1, Pallas kernels, total_call(): pl.pallas_call(functools.partial(total_kernel, skies), out_shape=(jax.Sha...  19.9 us
    pallas_call x1, Pallas kernels, send_call(): pl.pallas_call(send_kernel, out_shape=(jax.ShapeDtypeStruct((2 * GROUPS +...  12.9 us
    pallas_call x1, Pallas kernels, count_call(): pl.pallas_call(count_kernel, out_shape=jax.ShapeDtypeStruct((2 * SUBREGIO...  6.33 us

profile of v5, /device:TPU:4, one launch (start us, length us, event | category | flops | bytes accessed | tf_op | source)
XLA Modules:
  0.0 41.4 jit_solution(1640484920811862787)
XLA Ops:
  0.7 12.9 %shard_map.46 = (s32[64,128]{1,0:T(8,128)S(1)}, f32[289,8,128]{2,1,0:T(8,128)S(1)}, f32[4,24,8,128]{3,2,1,0:T(8,128)S(1)}) custom-call(s32[3,1,1,512]{3,2,1,0:T(1,128)} %coords_hbm.1, bf16[1,1,512]{2,1,0:T(2,128)(2,1)} %weight_hbm.1, s32[1,1]{1,0:T(1,128)S(6)} %copy.14.live_hbm), custom_call_target="tpu_custom_call" | custom-call | tf_op jit(solution)/shard_map/pallas_call | solution.py:271
  13.6 6.3 %shard_map.47.counts_ref = f32[16,208,256]{2,1,0:T(8,128)S(1)} custom-call(s32[64,128]{1,0:T(8,128)S(1)} %get-tuple-element.10.table_ref, f32[289,8,128]{2,1,0:T(8,128)S(1)} %get-tuple-element.11.rows_ref, f32[4,24,8,128]{3,2,1,0:T(8,128)S(1)} %get-tuple-element.12.own_ref), custom_call_target="tpu_custom_call" | custom-call | tf_op jit(solution)/shard_map/pallas_call | solution.py:443
  19.9 0.0 copy-start
  19.9 19.9 %shard_map.48 = (f32[64,128]{1,0:T(8,128)S(1)}, f32[8,128]{1,0:T(8,128)S(1)}) custom-call(f32[16,208,256]{2,1,0:T(8,128)S(1)} %shard_map.47.counts_ref), custom_call_target="tpu_custom_call" | custom-call | tf_op jit(solution)/shard_map/pallas_call | solution.py:518
  39.8 0.1 sub.11
  39.9 0.1 reshape.24
  40.0 0.1 slice.22
  40.1 0.1 copy.11
  40.3 0.1 reshape.26
  40.4 0.1 copy.12
  40.5 0.1 reshape.28
  40.6 0.1 reshape.29
  40.7 0.0 copy-done
  40.7 0.7 %multiply_bitcast_fusion = f32[1,8,600]{2,1,0:T(8,128)} fusion(f32[8,600]{1,0:T(8,128)S(1)} %reshape.26, f32[8,200]{1,0:T(8,128)S(1)} %bitcast.15, f32[600]{0:T(1024)S(1)} %copy-done), kind=kLoop, calls=%fused_computation.2 | loop fusion | flops 9600 | bytes 47200 | tf_op jit(solution)/shard_map/broadcast_in_dim | solution.py:560
  (3 shorter events, 0.0 us)
Async XLA Ops:
  19.9 20.8 %copy-start = (f32[600]{0:T(1024)S(1)}, f32[600]{0:T(1024)}, u32[]{:S(2)}) copy-start(f32[600]{0:T(1024)} %constant.5.clone) | copy-start | bytes 7204
